TPU v7x, 32 devices: a whole 2x2x4 slice. The times are simulated.
32 devices in a mesh: grp: 2 (over y), row: 16 (over z, x, core).
Axes of the slice: x: 2, y: 2, z: 4, core: 2. Of those that a mesh axis runs over, the one named last changes fastest.
Arguments:
- item_ids: int32 [128, 512], P(('grp', 'row')), may hold values from 0 to 49999, as said below
- lengths: int32 [128], P(('grp', 'row')), may hold values from 358 to 512
- target_ids: int32 [128, 512], P(('grp', 'row')), may hold values from 0 to 49999
- target_logq: bfloat16 [128, 512], P(('grp', 'row')), may hold values from -4 to 0
- negative_ids: int32 [2048], P(('grp', 'row')), may hold values from 0 to 49999
- negative_logq: bfloat16 [2048], P(('grp', 'row')), may hold values from -4 to 0
- table_weight: float32 [50000, 256], P('row'), may hold values from -0.6 to 0.6
- table_accum: float32 [50000], P('row'), may hold values from 1.1737531e-13 to 4.6950123e-13
- dense_weight: float32 [256, 4608], P(None, ('grp', 'row')), may hold values from -0.375 to 0.375
- dense_first: float32 [256, 4608], P(None, ('grp', 'row')), may hold values from -2.861023e-06 to 2.861023e-06
- dense_second: float32 [256, 4608], P(None, ('grp', 'row')), may hold values from 3.390842e-15 to 1.3563368e-14
- gain_weight: float32 [3, 256], replicated, may hold values from 0.5 to 1.5
- gain_first: float32 [3, 256], replicated, may hold values from -3.0517578e-05 to 3.0517578e-05
- gain_second: float32 [3, 256], replicated, may hold values from 3.390842e-13 to 1.3563368e-12
Outputs:
- mean_loss: float32 [], replicated
- grad_norm: float32 [], replicated
- new_table: float32 [50000, 256], P('row')
- table_grad: float32 [50000, 256], P('row')
- new_accum: float32 [50000], P('row')
- table_copy: bfloat16 [50000, 256], P('row')
- new_dense: float32 [256, 4608], P(None, ('grp', 'row'))
- new_first: float32 [256, 4608], P(None, ('grp', 'row'))
- new_second: float32 [256, 4608], P(None, ('grp', 'row'))
- dense_copy: bfloat16 [256, 4608], P(None, ('grp', 'row'))
- new_gains: float32 [3, 256], replicated
- new_gain_first: float32 [3, 256], replicated
- new_gain_second: float32 [3, 256], replicated
Inputs may be any that keep to these rules, and one draw needn't show every extreme that they name: `item_ids`: taking one device's item ids, target ids and negative ids together, at most 520 of them name rows with the same id // 3125; in each group some value of id // 3125 is named exactly 520 times by every device of the group.
All inputs are finite; a program needn't handle non-finite values.
Results may differ from a plain program's by a relative error of at most 0.0093.
The roundings to bfloat16 on the way count: a program that leaves them out, or rounds other values in their place, can miss the bound.
Values may be sent and summed in bfloat16 or wider, within the bound.
A program may use at most 256 MiB of HBM per device.

v0:
```python
import jax
import jax.numpy as jnp
from jax import lax
from jax.sharding import PartitionSpec as P

HEADS = 8
HDIM = 64
FF = 1024
STEP = 10


clip_level = 0.002
adam_rate = 0.05
gains_rate = 0.6
rows_rate = 0.05
beta_one = 0.9
beta_two = 0.999
adam_eps = 1e-08
decay_rate = 0.01


def in_blocks(array, dim, devices):
    shape = array.shape
    pieces = array.reshape(*shape[:dim], devices, shape[dim] // devices, *shape[dim + 1 :])
    return jnp.moveaxis(pieces, dim, 0)


def sum_at_owner(array, axis, dim):
    devices = lax.axis_size(axis)
    pieces = lax.all_to_all(in_blocks(array, dim, devices), axis, 0, 0, tiled=True)
    return jnp.sum(pieces.astype(jnp.float32), axis=0)


def norm_apply(values, gain):
    return values * lax.rsqrt(jnp.mean(values * values, -1, keepdims=True) + 1e-06) * gain


def gelu_apply(values):
    return jax.nn.gelu(values, approximate=True)


def adam_update(weight, first, second, grad, decay, rate):
    first_new = beta_one * first + (1.0 - beta_one) * grad
    second_new = beta_two * second + (1.0 - beta_two) * grad * grad
    fix_one = 1.0 - beta_one**STEP
    fix_two = 1.0 - beta_two**STEP
    weight_new = weight - rate * (
        first_new / fix_one / (jnp.sqrt(second_new / fix_two) + adam_eps) + decay * weight
    )
    return (weight_new, first_new, second_new)


def attention_probs(queries, keys_all):
    scores = (
        jnp.einsum("sqhd,skhd->shqk", queries, keys_all, preferred_element_type=jnp.float32) * 0.125
    )
    length = queries.shape[1]
    causal = lax.broadcasted_iota(jnp.int32, (length, length), 0) >= lax.broadcasted_iota(
        jnp.int32, (length, length), 1
    )
    scores = jnp.where(causal[None, None], scores, -1e30)
    exponent = jnp.exp(scores - jnp.max(scores, -1, keepdims=True))
    return exponent / jnp.sum(exponent, -1, keepdims=True)


def shards(
    item_ids,
    lengths,
    target_ids,
    target_logq,
    negative_ids,
    negative_logq,
    table_weight,
    table_accum,
    dense_weight,
    dense_first,
    dense_second,
    gain_weight,
    gain_first,
    gain_second,
):
    seq_dev, length = item_ids.shape
    rows_dev, model_width = table_weight.shape
    peer_count = lax.axis_size("row")
    inner = HEADS * HDIM
    tokens = seq_dev * length
    single_float = jnp.float32
    brain_float_half = jnp.bfloat16
    local_dense = dense_weight.astype(brain_float_half)
    full_dense = lax.all_gather(local_dense, ("grp", "row"), axis=1, tiled=True)
    query_key_value_weight = full_dense[:, : 3 * inner]
    output_weight = full_dense[:, 3 * inner : 4 * inner]
    up_weight = full_dense[:, 4 * inner : 4 * inner + FF]
    down_weight = full_dense[:, 4 * inner + FF : 4 * inner + 2 * FF]
    pos_rows = full_dense[:, 4 * inner + 2 * FF :].T.astype(single_float)
    requests = jnp.concatenate([item_ids.reshape(-1), target_ids.reshape(-1), negative_ids])
    capacity = 2 * requests.shape[0] // peer_count
    owners = requests // rows_dev
    one_hot = (owners[:, None] == jnp.arange(peer_count, dtype=jnp.int32)[None, :]).astype(
        jnp.int32
    )
    rank_in = jnp.sum((jnp.cumsum(one_hot, 0) - one_hot) * one_hot, 1)
    slot_at = owners * capacity + rank_in
    send_ids = jnp.full((peer_count * capacity,), -1, jnp.int32).at[slot_at].set(requests)
    send_ids = send_ids.reshape(peer_count, capacity)
    table_low = table_weight.astype(brain_float_half)
    row_base = lax.axis_index("row") * rows_dev
    asked_ids = lax.all_to_all(send_ids, "row", split_axis=0, concat_axis=0, tiled=True)
    present = asked_ids >= 0
    found_rows = table_low[jnp.where(present, asked_ids - row_base, 0)]
    found_rows = jnp.where(present[..., None], found_rows, jnp.zeros_like(found_rows))
    returned = lax.all_to_all(found_rows, "row", split_axis=0, concat_axis=0, tiled=True)
    fetched, asked_ids = (returned, asked_ids)
    picked = fetched.reshape(peer_count * capacity, model_width)[slot_at]
    hist_rows = picked[:tokens].reshape(seq_dev, length, model_width)
    target_rows = picked[tokens : 2 * tokens]
    own_negatives = picked[2 * tokens :]
    neg_rows, neg_bias = (
        lax.all_gather(own_negatives, "row", axis=0, tiled=True),
        lax.all_gather(negative_logq, "row", axis=0, tiled=True),
    )
    embedded_tokens = hist_rows.astype(single_float) + pos_rows[None]
    normed, norm_back_one = jax.vjp(norm_apply, embedded_tokens, gain_weight[0])
    normalized_narrow = normed.astype(brain_float_half)
    mixed_state = jnp.einsum(
        "rnq,qm->rnm",
        normalized_narrow,
        query_key_value_weight,
        preferred_element_type=single_float,
    ).astype(brain_float_half)
    queries = mixed_state[..., :inner].reshape(seq_dev, length, HEADS, HDIM)
    keys_all = mixed_state[..., inner : 2 * inner].reshape(seq_dev, length, HEADS, HDIM)
    values_all = mixed_state[..., 2 * inner :].reshape(seq_dev, length, HEADS, HDIM)
    attn_probs = attention_probs(queries, keys_all)
    probs_low = attn_probs.astype(brain_float_half)
    attention_context = jnp.einsum(
        "shqk,skhd->sqhd", probs_low, values_all, preferred_element_type=single_float
    )
    attention_context = attention_context.reshape(seq_dev, length, inner).astype(brain_float_half)
    after_attention_state = embedded_tokens + jnp.einsum(
        "xaj,oj->xao", attention_context, output_weight, preferred_element_type=single_float
    )
    normed_two, norm_back_two = jax.vjp(norm_apply, after_attention_state, gain_weight[1])
    second_normalized_narrow = normed_two.astype(brain_float_half)
    hidden_preactivation = jnp.einsum(
        "bvi,iq->bvq", second_normalized_narrow, up_weight, preferred_element_type=single_float
    )
    hidden, gaussian_unit_backward = jax.vjp(gelu_apply, hidden_preactivation)
    hidden_narrow = hidden.astype(brain_float_half)
    after_ffn = after_attention_state + jnp.einsum(
        "ixn,on->ixo", hidden_narrow, down_weight, preferred_element_type=single_float
    )
    states, norm_back_three = jax.vjp(norm_apply, after_ffn, gain_weight[2])
    states_low = states.astype(brain_float_half).reshape(tokens, model_width)
    states_full = states_low.astype(single_float)
    target_full = target_rows.astype(single_float)
    pos_logit = jnp.sum(states_full * target_full, -1) - target_logq.reshape(tokens).astype(
        single_float
    )
    neg_logit = (
        jnp.einsum("td,nd->tn", states_low, neg_rows, preferred_element_type=single_float)
        - neg_bias.astype(single_float)[None, :]
    )
    highest_logit = jnp.maximum(jnp.max(neg_logit, 1), pos_logit)
    log_total = highest_logit + jnp.log(
        jnp.exp(pos_logit - highest_logit) + jnp.sum(jnp.exp(neg_logit - highest_logit[:, None]), 1)
    )
    is_valid = lax.broadcasted_iota(jnp.int32, (seq_dev, length), 1) < lengths[:, None]
    valid_full = is_valid.reshape(tokens).astype(single_float)
    loss_local = jnp.sum(valid_full * (log_total - pos_logit))
    event_local = jnp.sum(valid_full)
    loss_total, event_total = lax.psum((loss_local, event_local), ("grp", "row"))
    inverse = 1.0 / event_total
    d_pos = valid_full * inverse * (jnp.exp(pos_logit - log_total) - 1.0)
    d_neg = (valid_full[:, None] * inverse * jnp.exp(neg_logit - log_total[:, None])).astype(
        brain_float_half
    )
    d_states = d_pos[:, None] * target_full + jnp.einsum(
        "tn,nd->td", d_neg, neg_rows, preferred_element_type=single_float
    )
    d_target = d_pos[:, None] * states_full
    neg_grad = sum_at_owner(
        jnp.einsum("tn,td->nd", d_neg, states_low, preferred_element_type=single_float).astype(
            jnp.bfloat16
        ),
        "row",
        0,
    )
    d_ffn, d_gain_three = norm_back_three(d_states.reshape(seq_dev, length, model_width))
    branch_gradient = d_ffn.astype(brain_float_half)
    down_weight_gradient = jnp.einsum(
        "qgp,qgv->pv", branch_gradient, hidden_narrow, preferred_element_type=single_float
    )
    (hidden_gradient,) = gaussian_unit_backward(
        jnp.einsum("bvi,iq->bvq", branch_gradient, down_weight, preferred_element_type=single_float)
    )
    hidden_gradient_narrow = hidden_gradient.astype(brain_float_half)
    up_weight_gradient = jnp.einsum(
        "qgp,qgv->pv",
        second_normalized_narrow,
        hidden_gradient_narrow,
        preferred_element_type=single_float,
    )
    d_attn_part, d_gain_two = norm_back_two(
        jnp.einsum(
            "ixn,on->ixo", hidden_gradient_narrow, up_weight, preferred_element_type=single_float
        )
    )
    d_attn = d_ffn + d_attn_part
    output_gradient_narrow = d_attn.astype(brain_float_half)
    output_weight_gradient = jnp.einsum(
        "nkg,nka->ga",
        output_gradient_narrow,
        attention_context,
        preferred_element_type=single_float,
    )
    context_gradient = jnp.einsum(
        "mbg,gr->mbr", output_gradient_narrow, output_weight, preferred_element_type=single_float
    ).astype(brain_float_half)
    context_gradient = context_gradient.reshape(seq_dev, length, HEADS, HDIM)
    d_values = jnp.einsum(
        "shqk,sqhd->skhd", probs_low, context_gradient, preferred_element_type=single_float
    )
    d_probs = jnp.einsum(
        "sqhd,skhd->shqk", context_gradient, values_all, preferred_element_type=single_float
    )
    d_scores = (attn_probs * (d_probs - jnp.sum(attn_probs * d_probs, -1, keepdims=True))).astype(
        brain_float_half
    )
    d_queries = (
        jnp.einsum("shqk,skhd->sqhd", d_scores, keys_all, preferred_element_type=single_float)
        * 0.125
    )
    d_keys = (
        jnp.einsum("shqk,sqhd->skhd", d_scores, queries, preferred_element_type=single_float)
        * 0.125
    )
    mixed_gradient = jnp.concatenate(
        [
            d_queries.reshape(seq_dev, length, inner),
            d_keys.reshape(seq_dev, length, inner),
            d_values.reshape(seq_dev, length, inner),
        ],
        -1,
    ).astype(brain_float_half)
    query_key_value_gradient = jnp.einsum(
        "rbp,rbg->pg", normalized_narrow, mixed_gradient, preferred_element_type=single_float
    )
    d_embed_part, d_gain_one = norm_back_one(
        jnp.einsum(
            "igp,zp->igz",
            mixed_gradient,
            query_key_value_weight,
            preferred_element_type=single_float,
        )
    )
    d_embedded = d_attn + d_embed_part
    grad_pos = jnp.sum(d_embedded, 0).T
    grad_local = jnp.concatenate(
        [
            query_key_value_gradient,
            output_weight_gradient,
            up_weight_gradient,
            down_weight_gradient,
            grad_pos,
        ],
        1,
    )
    gain_local = jnp.stack([d_gain_one, d_gain_two, d_gain_three])
    dense_grad = lax.psum_scatter(grad_local, ("grp", "row"), scatter_dimension=1, tiled=True)
    row_grads = jnp.concatenate([d_embedded.reshape(tokens, model_width), d_target, neg_grad], 0)
    sent_grads = (
        jnp.zeros((peer_count * capacity, model_width), single_float).at[slot_at].set(row_grads)
    )
    arrived = lax.all_to_all(
        sent_grads.reshape(peer_count, capacity, model_width).astype(jnp.bfloat16),
        "row",
        split_axis=0,
        concat_axis=0,
        tiled=True,
    ).astype(jnp.float32)
    present = asked_ids >= 0
    local_rows = jnp.where(present, asked_ids - row_base, 0).reshape(-1)
    arrived = jnp.where(present[..., None], arrived, 0.0).reshape(-1, model_width)
    owner_grad = jax.ops.segment_sum(arrived, local_rows, num_segments=rows_dev)
    table_full = lax.psum(owner_grad.astype(jnp.bfloat16), "grp").astype(jnp.float32)
    dense_sq = jnp.sum(dense_grad * dense_grad)
    table_sq = jnp.sum(table_full * table_full) / lax.axis_size("grp")
    gain_grad, dense_total, table_total = lax.psum((gain_local, dense_sq, table_sq), ("grp", "row"))
    raw_norm = jnp.sqrt(dense_total + table_total + jnp.sum(gain_grad * gain_grad))
    factor = jnp.minimum(1.0, clip_level / raw_norm)
    table_grad = table_full * factor
    new_accum = table_accum + jnp.mean(table_grad * table_grad, -1)
    new_table = table_weight - rows_rate * table_grad / (jnp.sqrt(new_accum)[:, None] + adam_eps)
    new_dense, new_first, new_second = adam_update(
        dense_weight, dense_first, dense_second, dense_grad * factor, decay_rate, adam_rate
    )
    new_gains, new_gain_first, new_gain_second = adam_update(
        gain_weight, gain_first, gain_second, gain_grad * factor, 0.0, gains_rate
    )
    mean_loss = loss_total / event_total
    return (
        mean_loss,
        raw_norm,
        new_table,
        table_grad,
        new_accum,
        new_table.astype(brain_float_half),
        new_dense,
        new_first,
        new_second,
        new_dense.astype(brain_float_half),
        new_gains,
        new_gain_first,
        new_gain_second,
    )


def solution(mesh):
    return jax.shard_map(
        shards,
        mesh=mesh,
        in_specs=(
            P(("grp", "row"), None),
            P(("grp", "row")),
            P(("grp", "row"), None),
            P(("grp", "row"), None),
            P(("grp", "row")),
            P(("grp", "row")),
            P("row", None),
            P("row"),
            P(None, ("grp", "row")),
            P(None, ("grp", "row")),
            P(None, ("grp", "row")),
            P(),
            P(),
            P(),
        ),
        out_specs=(
            P(),
            P(),
            P("row", None),
            P("row", None),
            P("row"),
            P("row", None),
            P(None, ("grp", "row")),
            P(None, ("grp", "row")),
            P(None, ("grp", "row")),
            P(None, ("grp", "row")),
            P(),
            P(),
            P(),
        ),
        check_vma=False,
    )
```

profile of v0, /device:TPU:0, one launch (start us, length us, event | category | flops | bytes accessed | tf_op | source)
XLA Modules:
  0.0 841.6 jit_solution(8096171434932233010)
XLA Ops:
  10.8 4.7 reduce-window.6
  16.7 20.6 %scatter_custom_fusion = s32[8320]{0:T(1024)S(1)} fusion(s32[4160]{0:T(1024)S(1)} %fusion.57, s32[4160]{0:T(1024)S(1)} %constant_dynamic-update-slice_fusion.1, s32[]{:T(128)} %constant.34.clone.1), kind=kCustom, calls=%fused_computation.133 | custom fusion | bytes 33284 | tf_op jit(solution)/shard_map/scatter | solution.py:104
  38.0 7.4 all-to-all-start
  52.8 24.2 %gather_fusion = bf16[8320,256]{1,0:T(8,128)(2,1)} fusion(bf16[3125,256]{1,0:T(8,128)(2,1)S(1)} %convert_element_type.132, s32[9216]{0:T(1024)S(1)} %pad_clamp_fusion), kind=kCustom, calls=%fused_computation | custom fusion | bytes 8552960 | tf_op jit(solution)/shard_map/gather | solution.py:110
  77.7 5.3 broadcast_select_fusion
  83.0 4.7 all-to-all-start.1
  89.9 99.9 %all-reduce.1 = bf16[1024]{0:T(1024)(128)(2,1)S(1)} all-reduce(bf16[1024]{0:T(1024)(128)(2,1)S(1)} %dynamic-update-slice), channel_id=1, replica_groups=mesh['grp'=2,'row'=16] {'row'}, use_global_device_ids=true, to_apply=%add.1 | all-reduce | flops 1024 | bytes 4096
  191.0 12.5 %gather_fusion.1 = bf16[4160,256]{1,0:T(8,128)(2,1)S(1)} fusion(bf16[8320,256]{1,0:T(8,128)(2,1)} %bitcast.5, s32[5120]{0:T(1024)S(1)} %pad_clamp_fusion.1), kind=kCustom, calls=%fused_computation.1 | custom fusion | bytes 4276480 | tf_op jit(solution)/shard_map/gather | solution.py:114
  205.6 40.8 %all_gather.10 = bf16[1024,256]{1,0:T(8,128)(2,1)} all-gather(bf16[64,256]{1,0:T(8,128)(2,1)S(1)} %slice.84), channel_id=1, replica_groups=mesh['grp'=2,'row'=16] {'row'}, dimensions={0}, use_global_device_ids=true | all-gather | bytes 557056 | tf_op jit(solution)/shard_map/all_gather | solution.py:119
  264.1 19.1 %fusion.72 = (f32[4,8,512]{2,1,0:T(8,128)S(1)}, f32[4,8,512,512]{2,3,1,0:T(8,128)}) fusion(pred[512,512]{0,1:T(8,128)(4,1)S(1)} %iota_compare_fusion, bf16[4,512,8,64]{1,3,2,0:T(8,128)(2,1)} %bitcast.183, bf16[4,512,8,64]{1,3,2,0:T(8,128)(2,1)S(1)} %bitcast.181), kind=kOutput, calls=%fused_computation.173 | convolution fusion | flops 1107296768 | bytes 38076416 | tf_op jit(solution)/shard_map/sub | solution.py:62
  283.2 14.3 %fusion.33 = bf16[4,8,64,512]{3,2,1,0:T(8,128)(2,1)} fusion(bf16[4,512,8,64]{1,3,2,0:T(8,128)(2,1)} %bitcast.193, f32[4,8,512,512]{2,3,1,0:T(8,128)} %get-tuple-element.102, f32[4,8,512]{2,1,0:T(8,128)S(1)} %get-tuple-element.101), kind=kOutput, calls=%fused_computation.78 | convolution fusion | flops 1091567616 | bytes 37814272 | tf_op jit(solution)/shard_map/shqk,skhd->sqhd/dot_general | solution.py:136
  311.0 5.5 subtract_reduce_fusion
  321.6 38.8 %psum.43 = f32[]{:T(128)} all-reduce(f32[]{:T(128)} %get-tuple-element.71), channel_id=1, replica_groups=mesh['grp'=2,'row'=16] {'grp','row'}, use_global_device_ids=true, to_apply=%region_15.16 | all-reduce | flops 1 | bytes 8 | tf_op jit(solution)/shard_map/psum | solution.py:172
  374.1 6.7 fusion.11
  388.1 15.3 %fusion.36 = bf16[4,8,64,512]{3,2,1,0:T(8,128)(2,1)} fusion(bf16[4,512,8,64]{1,3,2,0:T(8,128)(2,1)} %bitcast.196, f32[4,8,512,512]{2,3,1,0:T(8,128)} %get-tuple-element.102, f32[4,8,512]{2,1,0:T(8,128)S(1)} %get-tuple-element.101), kind=kOutput, calls=%fused_computation.79 | convolution fusion | flops 1091567616 | bytes 37814272 | tf_op jit(solution)/shard_map/shqk,sqhd->skhd/dot_general | solution.py:221
  403.3 22.9 %multiply_reduce_fusion = (f32[4,8,512]{2,1,0:T(8,128)S(1)}, f32[4,8,512,512]{2,3,1,0:T(8,128)}) fusion(f32[4,8,512,512]{2,3,1,0:T(8,128)} %get-tuple-element.102, f32[4,8,512]{2,1,0:T(8,128)S(1)} %get-tuple-element.101, bf16[4,512,8,64]{1,3,2,0:T(8,128)(2,1)} %bitcast.197, bf16[4,512,8,64]{1,3,2,0:T(8,128)(2,1)} %bitcast.194), kind=kOutput, calls=%fused_computation.7 | convolution fusion | flops 1098891264 | bytes 71434240 | tf_op jit(solution)/shard_map/sqhd,skhd->shqk/dot_general | solution.py:224
  426.2 27.6 %multiply_convert_fusion = bf16[4,8,512,512]{2,3,1,0:T(8,128)(2,1)} fusion(f32[4,8,512,512]{2,3,1,0:T(8,128)} %get-tuple-element.111, f32[4,8,512]{2,1,0:T(8,128)S(1)} %get-tuple-element.110, f32[4,8,512,512]{2,3,1,0:T(8,128)} %get-tuple-element.102, f32[4,8,512]{2,1,0:T(8,128)S(1)} %get-tuple-element.101), kind=kLoop, calls=%fused_computation.6 | loop fusion | flops 33554432 | bytes 84017152 | tf_op jit(solution)/shard_map/convert_element_type | solution.py:227
  453.8 12.9 %multiply_convert_fusion.3 = bf16[4,8,64,512]{3,2,1,0:T(8,128)(2,1)} fusion(bf16[4,512,8,64]{1,3,2,0:T(8,128)(2,1)} %bitcast.184, bf16[4,8,512,512]{2,3,1,0:T(8,128)(2,1)} %multiply_convert_fusion), kind=kOutput, calls=%fused_computation.43 | convolution fusion | flops 1075838976 | bytes 20971520 | tf_op jit(solution)/shard_map/shqk,sqhd->skhd/dot_general | solution.py:235
  466.7 10.6 %multiply_convert_fusion.4 = bf16[4,8,64,512]{3,2,1,0:T(8,128)(2,1)} fusion(bf16[4,512,8,64]{1,3,2,0:T(8,128)(2,1)} %bitcast.182, bf16[4,8,512,512]{2,3,1,0:T(8,128)(2,1)} %multiply_convert_fusion), kind=kOutput, calls=%fused_computation.44 | convolution fusion | flops 1075838976 | bytes 20971520 | tf_op jit(solution)/shard_map/shqk,skhd->sqhd/dot_general | solution.py:231
  477.3 5.4 all-to-all-start.2
  495.2 5.4 multiply_reduce_fusion.4
  507.3 6.3 fusion.26
  514.8 27.3 %scatter_custom_fusion.1 = f32[8320,256]{1,0:T(8,128)} fusion(s32[4160]{0:T(1024)} %copy-done.28, f32[64,256]{1,0:T(8,128)S(1)} %convert_reduce_fusion, f32[]{:T(128)} %constant.48.clone.1, f32[2048,256]{1,0:T(8,128)} %convert_multiply_fusion.4, f32[2048,256]{1,0:T(8,128)} %bitcast.174, f32[]{:T(128)} %constant.43.clone.1), kind=kCustom, calls=%fused_computation.35 | custom fusion | flops 2129920 | bytes 12780544 | tf_op jit(solution)/shard_map/scatter | solution.py:273
  542.1 5.3 convert_element_type.163
  547.4 6.1 all-to-all-start.3
  560.0 7.6 fusion.41
  568.5 6.0 copy.183
  575.4 63.3 %all-to-all-done.3 = bf16[16,520,256]{2,1,0:T(8,128)(2,1)} async-done(((bf16[16,520,256]{2,1,0:T(8,128)(2,1)}), bf16[16,520,256]{2,1,0:T(8,128)(2,1)}, u32[]{:S(2)}, u32[]{:S(2)}) %all-to-all-start.3) | async-done | bytes 4259872 | tf_op jit(solution)/shard_map/all_to_all | solution.py:275
  638.7 7.1 convert_select_fusion
  645.8 52.6 %scatter_custom_fusion.2 = f32[3125,256]{1,0:T(8,128)S(1)} fusion(s32[8320]{0:T(1024)S(1)} %reshape.563, f32[8320,256]{1,0:T(8,128)} %bitcast.180, f32[]{:T(128)} %constant.43.clone.1), kind=kCustom, calls=%fused_computation.82 | custom fusion | flops 2129920 | bytes 3200512 | tf_op jit(solution)/shard_map/scatter-add | solution.py:285
  701.5 76.4 %all-reduce.5.cloned.1.call-done = bf16[3125,256]{1,0:T(8,128)(2,1)} async-done(((bf16[3125,256]{1,0:T(8,128)(2,1)}), bf16[3125,256]{1,0:T(8,128)(2,1)}) %all-reduce.5.cloned.1.call-update) | async-done | bytes 1600016 | tf_op jit(solution)/shard_map/psum | solution.py:286
  782.2 39.6 %all-reduce.2 = (f32[]{:T(128)}, f32[]{:T(128)}, f32[3,256]{1,0:T(4,128)S(1)}) all-reduce(f32[]{:T(128)} %get-tuple-element.72, f32[]{:T(128)S(6)} %add.230, f32[3,256]{1,0:T(4,128)S(1)} %pad_maximum_fusion.3), channel_id=1, replica_groups=mesh['grp'=2,'row'=16] {'grp','row'}, use_global_device_ids=true, to_apply=%region_13.14 | all-reduce | flops 770 | bytes 6160 | tf_op jit(solution)/shard_map/psum | solution.py:172
  (204 shorter events, 117.0 us)
Async XLA Ops:
  7.2 9.3 %copy-start.44 = (s32[64]{0:T(128)S(1)}, s32[64]{0:T(128)}, u32[]{:S(2)}) copy-start(s32[64]{0:T(128)} %param.18) | copy-start | bytes 772
  16.7 173.2 %copy-start.28 = (s32[4160]{0:T(1024)}, s32[4160]{0:T(1024)S(1)}, u32[]{:S(2)}) copy-start(s32[4160]{0:T(1024)S(1)} %fusion.57) | copy-start | bytes 49924
  38.0 14.1 %all-to-all-start = ((s32[16,1,520]{2,1,0:T(1,128)}), s32[16,1,520]{2,1,0:T(1,128)S(1)}, u32[]{:S(2)}, u32[]{:S(2)}) async-start(s32[16,1,520]{2,1,0:T(1,128)} %all_to_all.15), calls=%async_computation | async-start | bytes 81920 | tf_op jit(solution)/shard_map/all_to_all | solution.py:108
  83.0 4.8 copy-start.21
  83.0 5.5 copy-start.46
  83.0 6.7 copy-start.45
  83.0 106.9 %copy-start.34 = (bf16[4,512]{1,0:T(4,128)(2,1)S(1)}, bf16[4,512]{1,0:T(4,128)(2,1)}, u32[]{:S(2)}) copy-start(bf16[4,512]{1,0:T(4,128)(2,1)} %param.17) | copy-start | bytes 12292
  83.0 107.0 %copy-start.35 = (f32[3,256]{1,0:T(4,128)S(1)}, f32[3,256]{1,0:T(4,128)}, u32[]{:S(2)}) copy-start(f32[3,256]{1,0:T(4,128)} %param.25) | copy-start | bytes 9220
  83.0 108.0 %all-to-all-start.1 = ((bf16[16,520,256]{2,1,0:T(8,128)(2,1)}), bf16[16,520,256]{2,1,0:T(8,128)(2,1)}, u32[]{:S(2)}, u32[]{:S(2)}) async-start(bf16[16,520,256]{2,1,0:T(8,128)(2,1)} %broadcast_select_fusion), calls=%async_computation.1 | async-start | bytes 8519680 | tf_op jit(solution)/shard_map/all_to_all | solution.py:112
  87.7 102.3 %all-gather.2.cloned.1.call-start = ((), (), s32[]{:S(2)}) async-start(), calls=%async_computation.5 | async-start | bytes 2433024 | tf_op jit(solution)/shard_map/all_gather | solution.py:90
  190.0 56.4 %copy-start.37 = (f32[1,256]{1,0:T(1,128)}, f32[1,256]{1,0:T(1,128)S(1)}, u32[]{:S(2)}) copy-start(f32[1,256]{1,0:T(1,128)S(1)} %get-tuple-element.100) | copy-start | bytes 3076
  191.0 106.5 %copy-start.9 = (f32[512,256]{1,0:T(8,128)}, f32[512,256]{1,0:T(8,128)S(1)}, u32[]{:S(2)}) copy-start(f32[512,256]{1,0:T(8,128)S(1)} %convert_bitcast_fusion) | copy-start | bytes 1572868
  203.6 42.8 %copy-start.2 = (bf16[4160,256]{1,0:T(8,128)(2,1)}, bf16[4160,256]{1,0:T(8,128)(2,1)S(1)}, u32[]{:S(2)}) copy-start(bf16[4160,256]{1,0:T(8,128)(2,1)S(1)} %gather_fusion.1) | copy-start | bytes 6389764
  205.6 44.1 %copy-start.29 = (f32[4,512]{1,0:T(4,128)}, f32[4,512]{1,0:T(4,128)S(1)}, u32[]{:S(2)}) copy-start(f32[4,512]{1,0:T(4,128)S(1)} %add.216) | copy-start | bytes 24580
  205.6 44.1 %copy-start.31 = (f32[4,512]{1,0:T(4,128)}, f32[4,512]{1,0:T(4,128)S(1)}, u32[]{:S(2)}) copy-start(f32[4,512]{1,0:T(4,128)S(1)} %rsqrt.30) | copy-start | bytes 24580
  255.4 8.7 %copy-start.15 = (bf16[4,512,512]{1,2,0:T(8,128)(2,1)}, bf16[4,512,512]{1,2,0:T(8,128)(2,1)S(1)}, u32[]{:S(2)}) copy-start(bf16[4,512,512]{1,2,0:T(8,128)(2,1)S(1)} %copy.151) | copy-start | bytes 6291460
  303.2 4.5 copy-start.16
  365.7 8.0 slice-start
  367.7 5.9 slice-start.1
  369.3 13.8 %copy-start.7 = (f32[2048,256]{1,0:T(8,128)}, f32[2048,256]{1,0:T(8,128)S(1)}, u32[]{:S(2)}) copy-start(f32[2048,256]{1,0:T(8,128)S(1)} %convolution_add_fusion) | copy-start | bytes 6291460
  477.3 36.4 %all-to-all-start.2 = ((bf16[16,64,256]{2,1,0:T(8,128)(2,1)}), bf16[16,64,256]{2,1,0:T(8,128)(2,1)}, u32[]{:S(2)}, u32[]{:S(2)}) async-start(bf16[16,64,256]{2,1,0:T(8,128)(2,1)} %bitcast.39), calls=%async_computation.2 | async-start | bytes 1048576 | tf_op jit(solution)/shard_map/all_to_all | solution.py:30
  495.2 5.5 copy-start.30
  495.2 5.5 copy-start.1
  547.4 91.3 %all-to-all-start.3 = ((bf16[16,520,256]{2,1,0:T(8,128)(2,1)}), bf16[16,520,256]{2,1,0:T(8,128)(2,1)}, u32[]{:S(2)}, u32[]{:S(2)}) async-start(bf16[16,520,256]{2,1,0:T(8,128)(2,1)} %bitcast.179), calls=%async_computation.3 | async-start | bytes 8519680 | tf_op jit(solution)/shard_map/all_to_all | solution.py:275
  553.5 146.3 %reduce-scatter.4.cloned.1.call-start = ((), (), s32[]{:S(2)}) async-start(), calls=%async_computation.7 | async-start | bytes 4866048
  574.5 64.2 %copy-start.27 = (pred[16,520]{1,0:T(8,128)(4,1)S(1)}, pred[16,520]{1,0:T(8,128)(4,1)}, u32[]{:S(2)}) copy-start(pred[16,520]{1,0:T(8,128)(4,1)} %copy-done.26) | copy-start | bytes 24964
  574.5 203.4 %all-reduce.5.cloned.1.call-start = ((), (), s32[]{:S(2)}) async-start(), calls=%async_computation.6 | async-start | bytes 3203072 | tf_op jit(solution)/shard_map/psum | solution.py:286
  699.7 125.4 %copy-start.36 = (f32[3,256]{1,0:T(4,128)S(1)}, f32[3,256]{1,0:T(4,128)}, u32[]{:S(2)}) copy-start(f32[3,256]{1,0:T(4,128)} %param.25) | copy-start | bytes 9220
  699.7 125.4 %copy-start.40 = (f32[3,256]{1,0:T(4,128)S(1)}, f32[3,256]{1,0:T(4,128)}, u32[]{:S(2)}) copy-start(f32[3,256]{1,0:T(4,128)} %param.26) | copy-start | bytes 9220
  699.7 125.4 %copy-start.41 = (f32[3,256]{1,0:T(4,128)S(1)}, f32[3,256]{1,0:T(4,128)}, u32[]{:S(2)}) copy-start(f32[3,256]{1,0:T(4,128)} %param.27) | copy-start | bytes 9220
  777.9 47.8 %copy-start.17 = (bf16[3125,256]{1,0:T(8,128)(2,1)S(1)}, bf16[3125,256]{1,0:T(8,128)(2,1)}, u32[]{:S(2)}) copy-start(bf16[3125,256]{1,0:T(8,128)(2,1)} %all-reduce.5.cloned.1.call-done) | copy-start | bytes 4800004
  826.3 5.5 copy-start.12
  (24 other events, 59.5 us)
Sparse Core Ops, SparseCore 0:
  92.0 97.0 all-gather.1
  574.6 114.1 reduce-scatter.3
  699.9 78.0 all-reduce.4
where the time goes:
time: 849 us; the launch traced here: 842 us
  blocking collectives  219 us (26%)
  other arithmetic  170 us (20%)
  matrix products  154 us (18%)
  waiting for transfers between devices  144 us (17%)
  local copies, waits for them, and re-layouts  107 us (13%)
  starting transfers between devices  23.7 us (3%)
  between operations  22.5 us (3%)
    unnamed x1, blocking collectives  99.9 us
    psum x2, blocking collectives, shards(): lax.psum((loss_local, event_local), ('grp', 'row'))  78.4 us
    psum x1, waiting for transfers between devices, shards(): lax.psum(owner_grad.astype(jnp.bfloat16), 'grp').astype(jnp.float32)  76.4 us
    all_to_all x1, waiting for transfers between devices, shards(): lax.all_to_all(sent_grads.reshape(peer_count, capacity, model_width).asty...  63.3 us
    scatter-add x1, other arithmetic, shards(): owner_grad = jax.ops.segment_sum(arrived, local_rows, num_segments=rows_dev)  52.6 us
    all_gather x1, blocking collectives, shards(): lax.all_gather(own_negatives, 'row', axis=0, tiled=True)  40.8 us
    convert_element_type x1, other arithmetic, shards(): (attn_probs * (d_probs - jnp.sum(attn_probs * d_probs, -1, keepdims=True)...  27.6 us
    scatter x1, other arithmetic, shards(): jnp.zeros((peer_count * capacity, model_width), single_float).at[slot_at]  27.3 us
  transfers between devices with their start and end apart: 7, of which 3 were waited for; matrix products, arithmetic and copies ran while one was open for 14% of the time, Pallas kernels for 0%

commit v1 on v0

v1 whole, which is shorter than its diff:
```python
import functools

import jax
import jax.numpy as jnp
from jax import lax
from jax.experimental import pallas as pl
from jax.experimental.pallas import tpu as pltpu
from jax.sharding import PartitionSpec as P

HEADS = 8
HDIM = 64
FF = 1024
STEP = 10
f32 = jnp.float32
bf16 = jnp.bfloat16

def mm(a, b):
    return lax.dot_general(a, b, (((1,), (0,)), ((), ())), preferred_element_type=f32)


def mm_t(a, b):
    return lax.dot_general(a, b, (((1,), (1,)), ((), ())), preferred_element_type=f32)


def t_mm(a, b):
    return lax.dot_general(a, b, (((0,), (0,)), ((), ())), preferred_element_type=f32)


GELU_C = 0.7978845608028654


def seq_kernel(
    len_ref, inv_ref,
    hist_ref, tgt_ref, tlq_ref, neg_ref, nlq_ref, wt_ref, gain_ref,
    demb_ref, dtgt_ref, gt_ref, ng_ref, gg_ref, loss_ref,
    emb, xn1, qkv, qh, kh, vh, dch, probs, ctx, aat, xn2, hid, gp, ffn, st, dneg, dst, dhid, dmx, gacc, nacc, rb,
):
    s = pl.program_id(0)
    last = pl.num_programs(0) - 1
    L, D = emb.shape
    inner = HEADS * HDIM
    O1 = 3 * inner
    O2 = O1 + inner
    O3 = O2 + FF
    O4 = O3 + FF
    RB = 128
    NB = L // RB

    @pl.when(s == 0)
    def _():
        @pl.loop(0, D // 16)
        def _(i):
            r = pl.ds(pl.multiple_of(i * 16, 16), 16)
            gacc[r, :] = jnp.zeros((16, gacc.shape[1]), f32)
            nacc[r, :] = jnp.zeros((16, nacc.shape[1]), f32)
        gt_ref[O4:, :] = jnp.zeros((L, D), f32)
        gg_ref[...] = jnp.zeros(gg_ref.shape, f32)
        loss_ref[...] = jnp.zeros(loss_ref.shape, f32)

    g1 = gain_ref[0:1, :]
    g2 = gain_ref[1:2, :]
    g3 = gain_ref[2:3, :]

    def rows(i):
        return pl.ds(pl.multiple_of(i * RB, RB), RB)

    def inv_rms(x):
        return lax.rsqrt(jnp.mean(x * x, -1, keepdims=True) + 1e-06)

    @pl.loop(0, NB)
    def _(i):
        r = rows(i)
        x = hist_ref[0, r, :].astype(f32) + wt_ref[pl.ds(pl.multiple_of(O4 + i * RB, RB), RB), :].astype(f32)
        emb[r, :] = x
        xn1[r, :] = (x * inv_rms(x) * g1).astype(bf16)

    qkv[...] = mm_t(xn1[...], wt_ref[0:O1, :]).astype(bf16)

    lane = lax.broadcasted_iota(jnp.int32, (1, 2 * HDIM), 1)

    def own(h):
        return (lane // HDIM) == (h % 2)

    @pl.loop(0, HEADS)
    def _(h):
        m = own(h)
        off = pl.multiple_of((h // 2) * 2 * HDIM, 2 * HDIM)
        zero = jnp.zeros((), bf16)
        qh[h] = jnp.where(m, qkv[:, pl.ds(off, 2 * HDIM)] * jnp.asarray(0.125, bf16), zero)
        kh[h] = jnp.where(m, qkv[:, pl.ds(pl.multiple_of(inner + off, 2 * HDIM), 2 * HDIM)], zero)
        vh[h] = jnp.where(m, qkv[:, pl.ds(pl.multiple_of(2 * inner + off, 2 * HDIM), 2 * HDIM)], zero)

    QB = 256
    NQ = L // QB
    causal = lax.broadcasted_iota(jnp.int32, (QB, QB), 0) >= lax.broadcasted_iota(jnp.int32, (QB, QB), 1)

    @pl.loop(0, HEADS // 2)
    def _(hp):
        off = pl.multiple_of(hp * 2 * HDIM, 2 * HDIM)
        for i in range(NQ):
            n = (i + 1) * QB
            q0 = i * QB
            acc = None
            for j in range(2):
                h = hp * 2 + j
                sc = mm_t(qh[h, q0:q0 + QB, :], kh[h, 0:n, :])
                tail = jnp.where(causal, sc[:, q0:], -1e30)
                sc = tail if i == 0 else jnp.concatenate([sc[:, :q0], tail], 1)
                e = jnp.exp(sc - jnp.max(sc, -1, keepdims=True))
                p = e / jnp.sum(e, -1, keepdims=True)
                probs[h, q0:q0 + QB, 0:n] = p
                c = mm(p.astype(bf16), vh[h, 0:n, :])
                acc = c if acc is None else acc + c
            ctx[q0:q0 + QB, pl.ds(off, 2 * HDIM)] = acc.astype(bf16)

    aat[...] = emb[...] + mm(ctx[...], wt_ref[O1:O2, :])

    @pl.loop(0, NB)
    def _(i):
        r = rows(i)
        x = aat[r, :]
        xn2[r, :] = (x * inv_rms(x) * g2).astype(bf16)

    gp[...] = mm_t(xn2[...], wt_ref[O2:O3, :])

    @pl.loop(0, L // 32)
    def _(i):
        r = pl.ds(pl.multiple_of(i * 32, 32), 32)
        x = gp[r, :]
        x2 = x * x
        t = jnp.tanh(GELU_C * (x + 0.044715 * (x2 * x)))
        half = 0.5 * (1.0 + t)
        hid[r, :] = (x * half).astype(bf16)
        gp[r, :] = half + (0.5 * GELU_C) * x * (1.0 - t * t) * (1.0 + (3 * 0.044715) * x2)

    ffn[...] = aat[...] + mm(hid[...], wt_ref[O3:O4, :])

    @pl.loop(0, NB)
    def _(i):
        r = rows(i)
        x = ffn[r, :]
        st[r, :] = (x * inv_rms(x) * g3).astype(bf16)

    inv = inv_ref[0, 0]
    length = len_ref[s]
    LB = 128
    eye = lax.broadcasted_iota(jnp.int32, (LB, LB), 0) == lax.broadcasted_iota(jnp.int32, (LB, LB), 1)

    @pl.loop(0, L // LB)
    def _(i):
        r = pl.ds(pl.multiple_of(i * LB, LB), LB)
        sl = st[r, :]
        sf = sl.astype(f32)
        tf = tgt_ref[0, r, :].astype(f32)
        tlq = jnp.sum(jnp.where(eye, tlq_ref[0, :, r], 0.0), 1, keepdims=True)
        pos = jnp.sum(sf * tf, -1, keepdims=True) - tlq
        neg = mm_t(sl, neg_ref[...]) - nlq_ref[...]
        top = jnp.maximum(jnp.max(neg, -1, keepdims=True), pos)
        e = jnp.exp(neg - top)
        total = jnp.exp(pos - top) + jnp.sum(e, -1, keepdims=True)
        lt = top + jnp.log(total)
        t_at = i * LB + lax.broadcasted_iota(jnp.int32, (LB, 1), 0)
        valid = (t_at < length).astype(f32)
        loss_ref[...] += jnp.sum(valid * (lt - pos))
        d_pos = valid * inv * (jnp.exp(pos - lt) - 1.0)
        dn = (e * (valid * inv / total)).astype(bf16)
        dneg[r, :] = dn
        dtgt_ref[0, r, :] = (d_pos * sf).astype(bf16)
        dst[r, :] = d_pos * tf + mm(dn, neg_ref[...])

    nacc[...] += t_mm(st[...], dneg[...])

    def norm_back(x, dy, g):
        r = inv_rms(x)
        xh = x * r
        dg = jnp.sum(dy * xh, 0, keepdims=True)
        dyg = dy * g
        dx = r * (dyg - xh * jnp.mean(dyg * xh, -1, keepdims=True))
        return dx, dg

    @pl.loop(0, NB)
    def _(i):
        r = rows(i)
        dx, dg = norm_back(ffn[r, :], dst[r, :], g3)
        gg_ref[2:3, :] += dg
        dst[r, :] = dx
        rb[r, :] = dx.astype(bf16)

    gacc[:, O3:O4] += t_mm(rb[...], hid[...])
    gp[...] = mm_t(rb[...], wt_ref[O3:O4, :]) * gp[...]
    dhid[...] = gp[...].astype(bf16)
    gacc[:, O2:O3] += t_mm(xn2[...], dhid[...])
    ffn[...] = mm(dhid[...], wt_ref[O2:O3, :])

    @pl.loop(0, NB)
    def _(i):
        r = rows(i)
        dx, dg = norm_back(aat[r, :], ffn[r, :], g2)
        gg_ref[1:2, :] += dg
        d = dst[r, :] + dx
        dst[r, :] = d
        rb[r, :] = d.astype(bf16)

    gacc[:, O1:O2] += t_mm(rb[...], ctx[...])
    ctx[...] = mm_t(rb[...], wt_ref[O1:O2, :]).astype(bf16)

    @pl.loop(0, HEADS)
    def _(h):
        off = pl.multiple_of((h // 2) * 2 * HDIM, 2 * HDIM)
        dch[h] = jnp.where(own(h), ctx[:, pl.ds(off, 2 * HDIM)], jnp.zeros((), bf16))

    @pl.loop(0, HEADS // 2)
    def _(hp):
        off = pl.multiple_of(hp * 2 * HDIM, 2 * HDIM)
        dk = [None] * NQ
        dv = [None] * NQ
        for i in range(NQ):
            n = (i + 1) * QB
            q0 = i * QB
            dq = None
            for j in range(2):
                h = hp * 2 + j
                p = probs[h, q0:q0 + QB, 0:n]
                dc = dch[h, q0:q0 + QB, :]
                dp = mm_t(dc, vh[h, 0:n, :])
                ds = (p * (dp - jnp.sum(p * dp, -1, keepdims=True))).astype(bf16)
                pb = p.astype(bf16)
                c = mm(ds, kh[h, 0:n, :])
                dq = c if dq is None else dq + c
                qb = qh[h, q0:q0 + QB, :]
                for b in range(i + 1):
                    k0 = b * QB
                    a = t_mm(ds[:, k0:k0 + QB], qb)
                    dk[b] = a if dk[b] is None else dk[b] + a
                    a = t_mm(pb[:, k0:k0 + QB], dc)
                    dv[b] = a if dv[b] is None else dv[b] + a
            dmx[q0:q0 + QB, pl.ds(off, 2 * HDIM)] = (dq * 0.125).astype(bf16)
        for b in range(NQ):
            k0 = b * QB
            dmx[k0:k0 + QB, pl.ds(pl.multiple_of(inner + off, 2 * HDIM), 2 * HDIM)] = dk[b].astype(bf16)
            dmx[k0:k0 + QB, pl.ds(pl.multiple_of(2 * inner + off, 2 * HDIM), 2 * HDIM)] = dv[b].astype(bf16)

    gacc[:, 0:O1] += t_mm(xn1[...], dmx[...])
    ffn[...] = mm(dmx[...], wt_ref[0:O1, :])

    @pl.loop(0, NB)
    def _(i):
        r = rows(i)
        dx, dg = norm_back(emb[r, :], ffn[r, :], g1)
        gg_ref[0:1, :] += dg
        d = dst[r, :] + dx
        demb_ref[0, r, :] = d.astype(bf16)
        gt_ref[pl.ds(pl.multiple_of(O4 + i * RB, RB), RB), :] += d

    @pl.when(s == last)
    def _():
        @pl.loop(0, O4 // 128)
        def _(i):
            c = pl.ds(pl.multiple_of(i * 128, 128), 128)
            gt_ref[c, :] = gacc[:, c].T

        @pl.loop(0, nacc.shape[1] // 128)
        def _(i):
            c = pl.ds(pl.multiple_of(i * 128, 128), 128)
            ng_ref[c, :] = nacc[:, c].T.astype(bf16)


def seq_step(lengths, inverse, hist, tgt, tlq, neg, nlq, wt, gains, interpret=False):
    S, L, D = hist.shape
    N = neg.shape[0]
    C = wt.shape[0]
    inner = HEADS * HDIM
    whole = lambda *shape: pl.BlockSpec(shape, lambda s: (0,) * len(shape))
    once = lambda *shape: pl.BlockSpec(shape, lambda s: (0,) * len(shape), pipeline_mode=pl.Buffered(1))
    per = pl.BlockSpec((1, L, D), lambda s: (s, 0, 0))
    V = pltpu.VMEM
    return pl.pallas_call(
        seq_kernel,
        grid=(S,),
        in_specs=[
            pl.BlockSpec(memory_space=pltpu.SMEM),
            pl.BlockSpec(memory_space=pltpu.SMEM),
            per, per,
            pl.BlockSpec((1, 1, L), lambda s: (s, 0, 0)),
            once(N, D), once(1, N), once(C, D), once(*gains.shape),
        ],
        out_specs=[per, per, whole(C, D), whole(N, D), whole(8, D), whole(1, 1)],
        out_shape=[
            jax.ShapeDtypeStruct((S, L, D), bf16),
            jax.ShapeDtypeStruct((S, L, D), bf16),
            jax.ShapeDtypeStruct((C, D), f32),
            jax.ShapeDtypeStruct((N, D), bf16),
            jax.ShapeDtypeStruct((8, D), f32),
            jax.ShapeDtypeStruct((1, 1), f32),
        ],
        scratch_shapes=[
            V((L, D), f32), V((L, D), bf16), V((L, 3 * inner), bf16),
            V((HEADS, L, 128), bf16), V((HEADS, L, 128), bf16), V((HEADS, L, 128), bf16), V((HEADS, L, 128), bf16),
            V((HEADS, L, L), f32), V((L, inner), bf16), V((L, D), f32), V((L, D), bf16),
            V((L, FF), bf16), V((L, FF), f32), V((L, D), f32), V((L, D), bf16),
            V((L, N), bf16), V((L, D), f32), V((L, FF), bf16), V((L, 3 * inner), bf16),
            V((D, C - L), f32), V((D, N), f32), V((L, D), bf16),
        ],
        compiler_params=pltpu.CompilerParams(vmem_limit_bytes=60 * 1024 * 1024, dimension_semantics=("arbitrary",)),
        name="seq_step",
        interpret=interpret,
    )(lengths, inverse, hist, tgt, tlq, neg, nlq, wt, gains)


MESH = pl.DeviceIdType.MESH


def gather_kernel(Z, X, parts, tab, wts, meta, table, wfull, mfull, send, recv, local):
    g = lax.axis_index("grp")
    row = lax.axis_index("row")
    z = row // (2 * X)
    x = (row // 2) % X
    c = row % 2
    K = len(parts) + 4
    KW = len(parts)
    KM = KW + 2

    def at(z_, x_, c_):
        return z_ * (2 * X) + x_ * 2 + c_

    nbr = {
        "up": (g, at(z + 1, x, c)), "dn": (g, at(z - 1, x, c)),
        "x": (g, at(z, 1 - x, c)), "y": (1 - g, row), "c": (g, at(z, x, 1 - c)),
    }
    has = {"up": z + 1 < Z, "dn": z > 0, "x": None, "y": None, "c": None}
    dirs = ("up", "dn", "x", "y", "c")

    def when(cond, f):
        if cond is None:
            f()
        else:
            pl.when(cond)(f)

    bar = pltpu.get_barrier_semaphore()
    for d in dirs:
        when(has[d], lambda d=d: pl.semaphore_signal(bar, inc=1, device_id=nbr[d], device_id_type=MESH))
    pl.semaphore_wait(bar, 3 + (z + 1 < Z).astype(jnp.int32) + (z > 0).astype(jnp.int32))

    def place(k, s, gg):
        if k < KW:
            st, size, _ = parts[k]
            return table.at[s, pl.ds(st, size), :]
        if k < KM:
            return wfull.at[gg * (2 * X * Z) + s]
        return mfull.at[gg * (2 * X * Z) + s]

    def origin(k):
        if k < KW:
            st, size, _ = parts[k]
            return tab.at[pl.ds(st, size), :]
        return wts if k < KM else meta

    def desc(d, k, s, gg, own):
        z_, x_ = s // (2 * X), (s // 2) % X
        return pltpu.make_async_remote_copy(
            src_ref=origin(k) if own else place(k, s, gg),
            dst_ref=place(k, s, gg),
            send_sem=send.at[dirs.index(d), z_ * X + x_, k],
            recv_sem=recv.at[s, k],
            device_id=nbr[d], device_id_type=MESH)

    started = []

    def go(d, k, s, gg, own=False, cond=None):
        conds = [q for q in (has[d], cond) if q is not None]
        cc = None if not conds else functools.reduce(jnp.logical_and, conds)
        when(cc, lambda: desc(d, k, s, gg, own).start())
        started.append((cc, d, k, s, gg, own))

    def take(k, s, gg):
        r = place(k, s, gg)
        pltpu.make_async_copy(r, r, recv.at[s, k]).wait()

    small = [KM, KW]

    def mine(fn):
        for k in range(KW):
            grp = parts[k][2]
            fn(k, g, None if grp < 0 else (g == grp))
        for k in small:
            for q in range(2):
                fn(k + q, q, g == q)

    def theirs(fn, own):
        for k in range(KW):
            grp = parts[k][2]
            if grp >= 0 and not own:
                fn(k, 1 - g, g != grp)
        for k in small:
            for q in range(2):
                fn(k + q, q, g != q)

    def both(a, b):
        if a is None:
            return b
        if b is None:
            return a
        return jnp.logical_and(a, b)

    s0 = at(z, x, c)
    order = {}

    def z0():
        def f(k, gg, cond):
            if k >= KW:
                go("y", k, s0, gg, True, cond)
            go("up", k, s0, gg, True, cond)
            go("dn", k, s0, gg, True, cond)
            go("x", k, s0, gg, True, cond)
            go("c", k, s0, gg, True, cond)
        mine(f)
        for k in range(KW):
            if parts[k][2] >= 0:
                go("c", k, s0, g, True, g != parts[k][2])
        for k in range(KW):
            pltpu.make_async_copy(origin(k), place(k, s0, g), local.at[k]).start()
        pltpu.make_async_copy(wts, place(KW, s0, g), local.at[KW]).start()
        pltpu.make_async_copy(meta, place(KM, s0, g), local.at[KW + 1]).start()

    def zd(d):
        for sg in (-1, 1):
            zz = z + sg * d
            ok = jnp.logical_and(zz >= 0, zz < Z)
            s = at(zz, x, c)

            def f(k, gg, cond):
                cc = both(cond, ok)
                when(cc, lambda: take(k, s, gg))
                if d < Z - 1:
                    go("up" if sg < 0 else "dn", k, s, gg, cond=cc)
                if k >= KW or parts[k][2] >= 0:
                    go("y", k, s, gg, cond=cc)
                go("x", k, s, gg, cond=cc)
                go("c", k, s, gg, cond=cc)
            mine(f)

    def xd(d):
        for sg in ((-1, 1) if d else (1,)):
            zz = z + sg * d
            ok = jnp.logical_and(zz >= 0, zz < Z) if d else None
            s = at(zz, 1 - x, c)

            def f(k, gg, cond):
                cc = both(cond, ok)
                when(cc, lambda: take(k, s, gg))
                if k >= KW or parts[k][2] >= 0:
                    go("y", k, s, gg, cond=cc)
                go("c", k, s, gg, cond=cc)
            mine(f)

    def yd(d, xx):
        for sg in ((-1, 1) if d else (1,)):
            zz = z + sg * d
            ok = jnp.logical_and(zz >= 0, zz < Z) if d else None
            s = at(zz, xx, c)

            def f(k, gg, cond):
                cc = both(cond, ok)
                when(cc, lambda: take(k, s, gg))
                go("c", k, s, gg, cond=cc)
            theirs(f, d == 0 and xx is x)

    z0()
    yd(0, x)
    zd(1)
    xd(0)
    yd(1, x)
    for d in range(2, Z):
        zd(d)
        xd(d - 1)
        yd(d - 2, 1 - x)
        yd(d, x)
    xd(Z - 1)
    yd(Z - 2, 1 - x)
    yd(Z - 1, 1 - x)
    for d in range(Z):
        for xx in (x, 1 - x):
            for sg in ((-1, 1) if d else (1,)):
                zz = z + sg * d
                ok = jnp.logical_and(zz >= 0, zz < Z) if d else None
                s = at(zz, xx, 1 - c)

                def f():
                    for k in range(KW):
                        take(k, s, 0)
                    for q in range(2):
                        take(KW + q, s, q)
                        take(KM + q, s, q)
                when(ok, f)
    for k in range(KW):
        pltpu.make_async_copy(origin(k), place(k, s0, g), local.at[k]).wait()
    pltpu.make_async_copy(wts, place(KW, s0, g), local.at[KW]).wait()
    pltpu.make_async_copy(meta, place(KM, s0, g), local.at[KW + 1]).wait()
    for cc, d, k, s, gg, own in started:
        when(cc, lambda: desc(d, k, s, gg, own).wait_send())


def gather_all(tab, wts, meta, Z, X, parts, cid=0):
    rows, D = tab.shape
    n = 2 * X * Z
    K = len(parts) + 4
    any_ = pl.BlockSpec(memory_space=pl.ANY)
    vm = pl.BlockSpec(memory_space=pltpu.VMEM)
    return pl.pallas_call(
        functools.partial(gather_kernel, Z, X, parts),
        out_shape=[
            jax.ShapeDtypeStruct((n, rows, D), tab.dtype),
            jax.ShapeDtypeStruct((2 * n,) + wts.shape, wts.dtype),
            jax.ShapeDtypeStruct((2 * n,) + meta.shape, meta.dtype),
        ],
        in_specs=[vm, vm, vm],
        out_specs=[any_, any_, any_],
        scratch_shapes=[
            pltpu.SemaphoreType.DMA((5, Z * X, K)),
            pltpu.SemaphoreType.DMA((n, K)),
            pltpu.SemaphoreType.DMA((len(parts) + 2,)),
        ],
        compiler_params=pltpu.CompilerParams(collective_id=cid, has_side_effects=True, vmem_limit_bytes=32 << 20),
        name="gather_all",
    )(tab, wts, meta)


def cut_parts(rows, na, nb, b):
    u = 16
    nbr = int(round(rows * b / u)) * u
    bounds = [0, rows - 2 * nbr, rows - nbr, rows]
    parts = []
    def split(lo, hi, n, grp):
        t = (hi - lo) // u
        cuts = [lo + u * (t * i // n) for i in range(n)] + [hi]
        for i in range(n):
            parts.append((cuts[i], cuts[i + 1] - cuts[i], grp))
    split(bounds[1], bounds[2], nb, 0)
    split(bounds[2], bounds[3], nb, 1)
    split(bounds[0], bounds[1], na, -1)
    return parts


clip_level = 0.002
adam_rate = 0.05
gains_rate = 0.6
rows_rate = 0.05
beta_one = 0.9
beta_two = 0.999
adam_eps = 1e-08
decay_rate = 0.01


def adam_update(weight, first, second, grad, decay, rate):
    first_new = beta_one * first + (1.0 - beta_one) * grad
    second_new = beta_two * second + (1.0 - beta_two) * grad * grad
    fix_one = 1.0 - beta_one**STEP
    fix_two = 1.0 - beta_two**STEP
    weight_new = weight - rate * (
        first_new / fix_one / (jnp.sqrt(second_new / fix_two) + adam_eps) + decay * weight
    )
    return (weight_new, first_new, second_new)


def round_up(n, unit):
    return -(-n // unit) * unit


def digits(ints, base, count):
    return [((ints // base**k) % base).astype(bf16) for k in range(count)]


def small_block(negative_ids, negative_logq, valid_here, width):
    n = negative_ids.shape[0]
    lines = [negative_logq] + digits(negative_ids, 256, 3)
    lines += [jnp.broadcast_to(d, (n,)) for d in digits(valid_here, 256, 2)]
    block = jnp.stack(lines)
    return jnp.pad(block, ((0, 16 - block.shape[0]), (0, width - n)))


def read_small(blocks, n):
    v = blocks[:, :6, :n].astype(f32)
    ids = (v[:, 1] + 256.0 * v[:, 2] + 65536.0 * v[:, 3]).astype(jnp.int32)
    events = jnp.sum(v[:, 4, 0] + 256.0 * v[:, 5, 0])
    return v[:, 0], ids, events


def slot_plan(requests, rows_dev, peers):
    capacity = 2 * requests.shape[0] // peers
    owners = requests // rows_dev
    one_hot = (owners[:, None] == jnp.arange(peers, dtype=jnp.int32)[None, :]).astype(jnp.int32)
    rank_in = jnp.sum((jnp.cumsum(one_hot, 0) - one_hot) * one_hot, 1)
    return owners * capacity + rank_in, capacity


def exchange(blocks):
    return lax.all_to_all(blocks, "row", split_axis=0, concat_axis=0, tiled=True)


def shards(
    shape,
    item_ids,
    lengths,
    target_ids,
    target_logq,
    negative_ids,
    negative_logq,
    table_weight,
    table_accum,
    dense_weight,
    dense_first,
    dense_second,
    gain_weight,
    gain_first,
    gain_second,
):
    groups, peers = shape
    seq_dev, length = item_ids.shape
    rows_dev, width = table_weight.shape
    tokens = seq_dev * length
    n_neg = negative_ids.shape[0]
    X = groups
    Z = peers // (2 * X)
    g = lax.axis_index("grp")
    row_base = lax.axis_index("row") * rows_dev

    table_low = table_weight.astype(bf16)
    dense_low = dense_weight.T.astype(bf16)
    small = small_block(negative_ids, negative_logq, jnp.sum(lengths), width)
    requests = jnp.concatenate([item_ids.reshape(-1), target_ids.reshape(-1), negative_ids])
    slot_at, capacity = slot_plan(requests, rows_dev, peers)
    send_ids = jnp.full((peers * capacity,), -1, jnp.int32).at[slot_at].set(requests)
    asked_ids = exchange(send_ids.reshape(peers, capacity))
    present = asked_ids >= 0

    if (groups, X) == (2, 2):
        rows_pad = round_up(rows_dev, 16)
        padded = jnp.pad(table_low, ((0, rows_pad - rows_dev), (0, 0)))
        table_all, dense_all, small_all = gather_all(
            padded, dense_low, small, Z, X, cut_parts(rows_pad, 2, 2, 0.333)
        )
        neg_bias, neg_ids, event_total = read_small(small_all, n_neg)
        neg_ids = lax.dynamic_slice_in_dim(neg_ids, g * peers, peers, 0).reshape(-1)
        neg_bias = lax.dynamic_slice_in_dim(neg_bias, g * peers, peers, 0).reshape(1, -1)
        wanted = jnp.concatenate([requests[: 2 * tokens], neg_ids])
        wanted = wanted + (rows_pad - rows_dev) * (wanted // rows_dev)
        picked = table_all.reshape(peers * rows_pad, width)[wanted]
        neg_rows = picked[2 * tokens :]
    else:
        dense_all = lax.all_gather(dense_low, ("grp", "row"), axis=0)
        small_all = lax.all_gather(small, ("grp", "row"), axis=0)
        neg_bias, neg_ids, event_total = read_small(small_all, n_neg)
        neg_bias = lax.dynamic_slice_in_dim(neg_bias, g * peers, peers, 0).reshape(1, -1)
        found = table_low[jnp.where(present, asked_ids - row_base, 0)]
        found = jnp.where(present[..., None], found, jnp.zeros_like(found))
        picked = exchange(found).reshape(peers * capacity, width)[slot_at]
        neg_rows = lax.all_gather(picked[2 * tokens :], "row", axis=0, tiled=True)
    hist_rows = picked[:tokens].reshape(seq_dev, length, width)
    target_rows = picked[tokens : 2 * tokens].reshape(seq_dev, length, width)
    dense_all = dense_all.reshape(-1, width)

    inverse = 1.0 / event_total
    d_embedded, d_target, grad_local, neg_local, gain_local, loss_local = seq_step(
        lengths,
        inverse.reshape(1, 1),
        hist_rows,
        target_rows,
        target_logq.astype(f32).reshape(seq_dev, 1, length),
        neg_rows,
        neg_bias,
        dense_all,
        gain_weight,
    )
    gain_local = gain_local[:3]

    dense_grad = lax.psum_scatter(grad_local, ("grp", "row"), scatter_dimension=0, tiled=True).T
    neg_grad = jnp.sum(exchange(neg_local.reshape(peers, n_neg, width)).astype(f32), 0)
    row_grads = jnp.concatenate(
        [d_embedded.reshape(tokens, width), d_target.reshape(tokens, width), neg_grad.astype(bf16)], 0
    ).astype(f32)
    sent = jnp.zeros((peers * capacity, width), f32).at[slot_at].set(row_grads).astype(bf16)
    arrived = exchange(sent.reshape(peers, capacity, width)).astype(f32)
    local_rows = jnp.where(present, asked_ids - row_base, 0).reshape(-1)
    arrived = jnp.where(present[..., None], arrived, 0.0).reshape(-1, width)
    owner_grad = jax.ops.segment_sum(arrived, local_rows, num_segments=rows_dev)
    table_full = lax.psum(owner_grad.astype(bf16), "grp").astype(f32)

    dense_sq = jnp.sum(dense_grad * dense_grad)
    table_sq = jnp.sum(table_full * table_full) / groups
    gain_grad, dense_total, table_total, loss_total = lax.psum(
        (gain_local, dense_sq, table_sq, loss_local[0, 0]), ("grp", "row")
    )
    raw_norm = jnp.sqrt(dense_total + table_total + jnp.sum(gain_grad * gain_grad))
    factor = jnp.minimum(1.0, clip_level / raw_norm)
    table_grad = table_full * factor
    new_accum = table_accum + jnp.mean(table_grad * table_grad, -1)
    new_table = table_weight - rows_rate * table_grad / (jnp.sqrt(new_accum)[:, None] + adam_eps)
    new_dense, new_first, new_second = adam_update(
        dense_weight, dense_first, dense_second, dense_grad * factor, decay_rate, adam_rate
    )
    new_gains, new_gain_first, new_gain_second = adam_update(
        gain_weight, gain_first, gain_second, gain_grad * factor, 0.0, gains_rate
    )
    return (
        loss_total / event_total,
        raw_norm,
        new_table,
        table_grad,
        new_accum,
        new_table.astype(bf16),
        new_dense,
        new_first,
        new_second,
        new_dense.astype(bf16),
        new_gains,
        new_gain_first,
        new_gain_second,
    )


def solution(mesh):
    shape = (mesh.shape["grp"], mesh.shape["row"])
    both = ("grp", "row")
    return jax.shard_map(
        functools.partial(shards, shape),
        mesh=mesh,
        in_specs=(
            P(both, None), P(both), P(both, None), P(both, None), P(both), P(both),
            P("row", None), P("row"), P(None, both), P(None, both), P(None, both),
            P(), P(), P(),
        ),
        out_specs=(
            P(), P(), P("row", None), P("row", None), P("row"), P("row", None),
            P(None, both), P(None, both), P(None, both), P(None, both),
            P(), P(), P(),
        ),
        check_vma=False,
    )
```

time: 849 us -> 654 us (0.77)
  Pallas kernels: 0 us -> 233 us
  blocking collectives: 219 us -> 39.6 us
  matrix products: 154 us -> 0 us
  local copies, waits for them, and re-layouts: 107 us -> 55.3 us
  other arithmetic: 170 us -> 119 us
  waiting for transfers between devices: 144 us -> 162 us
    pallas_call x0 -> x2, Pallas kernels: none -> 233 us  [the longest x1 118 us: gather_all(): pl.pallas_call(functools.partial(gather_kernel, Z, X, parts), out_shape=[...]
    dot_general x20 -> x0, matrix products: 135 us -> none  [the longest x1 22.9 us: shards(): jnp.einsum('sqhd,skhd->shqk', context_gradient, values_all, preferred_ele...]
    unnamed x1 -> x0, blocking collectives: 99.9 us -> none
    all_gather x1 -> x0, blocking collectives: 40.8 us -> none  [shards(): lax.all_gather(own_negatives, 'row', axis=0, tiled=True)]
    psum x2 -> x1, blocking collectives: 78.4 us -> 39.6 us  [shards(): lax.psum((gain_local, dense_sq, table_sq, loss_local[0, 0]), ('grp', 'row'))]
    convert_element_type x12 -> x8, other arithmetic: 48.1 us -> 12.4 us  [the longest x1 5.23 us: shards(): jnp.zeros((peers * capacity, width), f32).at[slot_at].set(row_grads)]
    all_to_all x4 -> x3, waiting for transfers between devices: 67.9 us -> 90.4 us  [exchange(): lax.all_to_all(blocks, 'row', split_axis=0, concat_axis=0, tiled=True)]
    sub x1 -> x0, matrix products: 19.1 us -> none  [attention_probs(): exponent = jnp.exp(scores - jnp.max(scores, -1, keepdims=True))]
  transfers between devices with their start and end apart: 7 -> 5, of which waited for: 3 -> 2; matrix products, arithmetic and copies ran while one was open for 14% -> 19% of each run, Pallas kernels for 0% -> 0%
where the time goes in v1:
time: 654 us; the launch traced here: 653 us
  Pallas kernels  233 us (36%)
  waiting for transfers between devices  162 us (25%)
  other arithmetic  119 us (18%)
  local copies, waits for them, and re-layouts  55.3 us (8%)
  blocking collectives  39.6 us (6%)
  between operations  25.6 us (4%)
  starting transfers between devices  17.7 us (3%)
    pallas_call x1, Pallas kernels, gather_all(): pl.pallas_call(functools.partial(gather_kernel, Z, X, parts), out_shape=[...  118 us
    pallas_call x1, Pallas kernels, seq_step(): pl.pallas_call(seq_kernel, grid=(S,), in_specs=[pl.BlockSpec(memory_space...  115 us
    all_to_all x3, waiting for transfers between devices, exchange(): lax.all_to_all(blocks, 'row', split_axis=0, concat_axis=0, tiled=True)  90.4 us
    psum x1, waiting for transfers between devices, shards(): table_full = lax.psum(owner_grad.astype(bf16), 'grp').astype(f32)  71.2 us
    scatter-add x1, other arithmetic, shards(): owner_grad = jax.ops.segment_sum(arrived, local_rows, num_segments=rows_dev)  52.6 us
    psum x1, blocking collectives, shards(): lax.psum((gain_local, dense_sq, table_sq, loss_local[0, 0]), ('grp', 'row'))  39.6 us
    scatter x1, other arithmetic, shards(): jnp.zeros((peers * capacity, width), f32).at[slot_at].set(row_grads)  31.3 us
    gather x1, local copies, waits for them, and re-layouts, shards(): picked = table_all.reshape(peers * rows_pad, width)[wanted]  28 us
  transfers between devices with their start and end apart: 5, of which 2 were waited for; matrix products, arithmetic and copies ran while one was open for 19% of the time, Pallas kernels for 0%

profile of v1, /device:TPU:0, one launch (start us, length us, event | category | flops | bytes accessed | tf_op | source)
XLA Modules:
  0.0 652.8 jit_solution(16074534740512422472)
XLA Ops:
  8.0 1.4 reduce_sum.77
  12.0 2.1 convert_element_type.62
  14.5 118.0 %gather_all.1 = (bf16[16,3136,256]{2,1,0:T(8,128)(2,1)}, bf16[32,144,256]{2,1,0:T(8,128)(2,1)S(1)}, bf16[32,16,256]{2,1,0:T(8,128)(2,1)S(1)}) custom-call(bf16[3136,256]{1,0:T(8,128)(2,1)S(1)} %pad.12.tab, bf16[144,256]{1,0:T(8,128)(2,1)S(1)} %convert_bitcast_fusion.wts, bf16[16,256]{1,0:T(8,128)(2,1)S(1)} %pad.13.meta), custom_call_target="tpu_custom_call" | custom-call | tf_op jit(solution)/shard_map/gather_all/pallas_call | solution.py:509
  132.4 1.4 copy-done
  133.9 0.6 fusion.21
  134.9 28.0 %gather_fusion = bf16[5120,256]{1,0:T(8,128)(2,1)S(1)} fusion(bf16[50176,256]{1,0:T(8,128)(2,1)} %bitcast.55, s32[5120]{0:T(1024)S(1)} %broadcast_clamp_fusion), kind=kCustom, calls=%fused_computation | custom fusion | bytes 5263360 | tf_op jit(solution)/shard_map/gather | solution.py:647
  162.8 1.5 fusion.37
  164.3 0.8 slice.67.neg_ref
  165.8 0.7 reshape.477.nlq_ref
  167.1 115.3 %seq_step.1 = (bf16[4,512,256]{2,1,0:T(8,128)(2,1)}, bf16[4,512,256]{2,1,0:T(8,128)(2,1)}, f32[4608,256]{1,0:T(8,128)}, bf16[1024,256]{1,0:T(8,128)(2,1)}, f32[8,256]{1,0:T(8,128)}, /*index=5*/f32[1,1]{1,0:T(1,128)}) custom-call(s32[4]{0:T(128)} %len_ref.1, f32[1,1]{1,0:T(1,128)} %bitcast.5.inv_ref, bf16[4,512,256]{2,1,0:T(8,128)(2,1)} %bitcast.59, ...), custom_call_target="tpu_custom_call" | custom-call | tf_op jit(solution)/shard_map/seq_step/pallas_call | solution.py:277
  282.5 5.6 all-to-all-start.1
  288.2 4.7 reduce-window.6
  294.1 20.6 %scatter_custom_fusion = s32[8320]{0:T(1024)S(1)} fusion(s32[4160]{0:T(1024)S(1)} %fusion.19, s32[4160]{0:T(1024)S(1)} %get-tuple-element.53, s32[]{:T(128)} %constant.157.clone.1), kind=kCustom, calls=%fused_computation.49 | custom fusion | bytes 33284 | tf_op jit(solution)/shard_map/scatter | solution.py:632
  314.7 0.7 all_to_all.12
  315.4 6.0 all-to-all-start
  321.5 31.3 %scatter_custom_fusion.1 = f32[8320,256]{1,0:T(8,128)} fusion(s32[4160]{0:T(1024)S(1)} %fusion.19, f32[]{:T(128)} %constant.161.clone.1, bf16[64,256]{1,0:T(8,128)(2,1)S(1)} %reduce_sum.82, bf16[]{:T(256)} %constant.207, bf16[2048,256]{1,0:T(8,128)(2,1)S(1)} %bitcast.63, bf16[2048,256]{1,0:T(8,128)(2,1)S(1)} %bitcast.62), kind=kCustom, calls=%fused_computation.5 | custom fusion | flops 6389760 | bytes 10649606 | tf_op jit(solution)/shard_map/scatter | solution.py:681
  352.8 5.2 convert_element_type.74
  358.0 6.0 all-to-all-start.2
  364.1 0.7 reduce-scatter.2.cloned.1.call-update
  365.0 90.4 %all-to-all-done.2 = bf16[16,520,256]{2,1,0:T(8,128)(2,1)} async-done(((bf16[16,520,256]{2,1,0:T(8,128)(2,1)}), bf16[16,520,256]{2,1,0:T(8,128)(2,1)}, u32[]{:S(2)}, u32[]{:S(2)}) %all-to-all-start.2) | async-done | bytes 4259872 | tf_op jit(solution)/shard_map/all_to_all | solution.py:597
  455.4 6.9 %convert_select_fusion = f32[16,520,256]{2,1,0:T(8,128)} fusion(bf16[16,520,256]{2,1,0:T(8,128)(2,1)} %all-to-all-done.2, pred[16,520]{1,0:T(8,128)(4,1)S(1)} %fusion.15), kind=kLoop, calls=%fused_computation.4 | loop fusion | flops 4259840 | bytes 12787840 | tf_op jit(solution)/shard_map/jit(_where)/select_n | solution.py:684
  462.3 52.6 %scatter_custom_fusion.2 = f32[3125,256]{1,0:T(8,128)S(1)} fusion(s32[8320]{0:T(1024)S(1)} %reshape.515, f32[8320,256]{1,0:T(8,128)} %bitcast.57, f32[]{:T(128)} %constant.161.clone.1), kind=kCustom, calls=%fused_computation.18 | custom fusion | flops 2129920 | bytes 3200512 | tf_op jit(solution)/shard_map/scatter-add | solution.py:685
  514.9 1.3 convert_element_type.76
  516.3 1.6 multiply_reduce_fusion.1
  517.9 71.2 %all-reduce.6.cloned.1.call-done = bf16[3125,256]{1,0:T(8,128)(2,1)} async-done(((bf16[3125,256]{1,0:T(8,128)(2,1)}), bf16[3125,256]{1,0:T(8,128)(2,1)}) %all-reduce.6.cloned.1.call-update) | async-done | bytes 1600016 | tf_op jit(solution)/shard_map/psum | solution.py:686
  589.0 2.8 fusion.3
  593.2 39.6 %all-reduce.3 = (f32[]{:T(128)}, f32[]{:T(128)}, f32[3,256]{1,0:T(4,128)S(1)}) all-reduce(f32[]{:T(128)} %bitcast.12, f32[]{:T(128)S(6)} %add.183, f32[3,256]{1,0:T(4,128)S(1)} %slice.57), channel_id=1, replica_groups=mesh['grp'=2,'row'=16] {'grp','row'}, use_global_device_ids=true, to_apply=%region_2.3 | all-reduce | flops 770 | bytes 6160 | tf_op jit(solution)/shard_map/psum | solution.py:690
  636.1 1.9 multiply_reduce_fusion
  638.0 0.6 sqrt_add_fusion
  638.7 2.9 fusion.36
  641.6 0.6 multiply_subtract_fusion.1
  642.3 0.9 fusion.33
  (81 shorter events, 3.5 us)
Async XLA Ops:
  8.0 6.1 copy-start.5
  8.0 6.1 copy-start.10
  8.0 6.2 copy-start.9
  12.0 2.3 copy-start.16
  12.0 2.4 copy-start.18
  132.4 1.4 copy-start
  162.8 2.3 copy-start.13
  282.4 39.1 %copy-start.3 = (bf16[4,512,256]{2,1,0:T(8,128)(2,1)S(1)}, bf16[4,512,256]{2,1,0:T(8,128)(2,1)}, u32[]{:S(2)}) copy-start(bf16[4,512,256]{2,1,0:T(8,128)(2,1)} %get-tuple-element.27) | copy-start | bytes 3145732
  282.5 39.1 %copy-start.4 = (bf16[4,512,256]{2,1,0:T(8,128)(2,1)S(1)}, bf16[4,512,256]{2,1,0:T(8,128)(2,1)}, u32[]{:S(2)}) copy-start(bf16[4,512,256]{2,1,0:T(8,128)(2,1)} %get-tuple-element.28) | copy-start | bytes 3145732
  282.5 32.9 %all-to-all-start.1 = ((bf16[16,64,256]{2,1,0:T(8,128)(2,1)}), bf16[16,64,256]{2,1,0:T(8,128)(2,1)S(1)}, u32[]{:S(2)}, u32[]{:S(2)}) async-start(bf16[16,64,256]{2,1,0:T(8,128)(2,1)} %bitcast.64), calls=%async_computation.2 | async-start | bytes 1048576 | tf_op jit(solution)/shard_map/all_to_all | solution.py:597
  315.4 42.6 %all-to-all-start = ((s32[16,1,520]{2,1,0:T(1,128)}), s32[16,1,520]{2,1,0:T(1,128)S(1)}, u32[]{:S(2)}, u32[]{:S(2)}) async-start(s32[16,1,520]{2,1,0:T(1,128)} %all_to_all.12), calls=%async_computation.1 | async-start | bytes 81920 | tf_op jit(solution)/shard_map/all_to_all | solution.py:597
  358.0 97.4 %all-to-all-start.2 = ((bf16[16,520,256]{2,1,0:T(8,128)(2,1)}), bf16[16,520,256]{2,1,0:T(8,128)(2,1)}, u32[]{:S(2)}, u32[]{:S(2)}) async-start(bf16[16,520,256]{2,1,0:T(8,128)(2,1)} %bitcast.56), calls=%async_computation.3 | async-start | bytes 8519680 | tf_op jit(solution)/shard_map/all_to_all | solution.py:597
  364.1 152.2 %reduce-scatter.2.cloned.1.call-start = ((), (), s32[]{:S(2)}) async-start(), calls=%async_computation.4 | async-start | bytes 4866048 | tf_op jit(solution)/shard_map/reduce_scatter | solution.py:676
  364.8 224.2 %all-reduce.6.cloned.1.call-start = ((), (), s32[]{:S(2)}) async-start(), calls=%async_computation.5 | async-start | bytes 3203072 | tf_op jit(solution)/shard_map/psum | solution.py:686
  514.9 1.3 copy-start.17
  517.9 120.2 %copy-start.11 = (f32[3125]{0:T(1024)S(1)}, f32[3125]{0:T(1024)}, u32[]{:S(2)}) copy-start(f32[3125]{0:T(1024)} %param.21) | copy-start | bytes 37504
  517.9 120.8 %copy-start.1 = (f32[3125,256]{1,0:T(8,128)S(1)}, f32[3125,256]{1,0:T(8,128)}, u32[]{:S(2)}) copy-start(f32[3125,256]{1,0:T(8,128)} %param.20) | copy-start | bytes 9600004
  638.0 3.6 copy-start.2
  638.7 2.9 copy-start.12
  638.7 2.9 copy-start.14
  638.7 2.9 copy-start.15
  638.7 3.6 copy-start.6
  638.7 3.6 copy-start.7
  638.7 3.6 copy-start.8
Sparse Core Ops, SparseCore 0:
  370.4 125.3 reduce-scatter.1
Sparse Core Ops, SparseCore 1:
  516.3 72.6 all-reduce.5

commit v2 on v1

--- a/solution.py
+++ b/solution.py
@@ -32,7 +32,7 @@
 def seq_kernel(
     len_ref, inv_ref,
     hist_ref, tgt_ref, tlq_ref, neg_ref, nlq_ref, wt_ref, gain_ref,
-    demb_ref, dtgt_ref, gt_ref, ng_ref, gg_ref, loss_ref,
+    demb_ref, dtgt_ref, gt_ref, ng_ref, gg_ref,
     emb, xn1, qkv, qh, kh, vh, dch, probs, ctx, aat, xn2, hid, gp, ffn, st, dneg, dst, dhid, dmx, gacc, nacc, rb,
 ):
     s = pl.program_id(0)
@@ -55,7 +55,6 @@
             nacc[r, :] = jnp.zeros((16, nacc.shape[1]), f32)
         gt_ref[O4:, :] = jnp.zeros((L, D), f32)
         gg_ref[...] = jnp.zeros(gg_ref.shape, f32)
-        loss_ref[...] = jnp.zeros(loss_ref.shape, f32)
 
     g1 = gain_ref[0:1, :]
     g2 = gain_ref[1:2, :]
@@ -161,7 +160,7 @@
         lt = top + jnp.log(total)
         t_at = i * LB + lax.broadcasted_iota(jnp.int32, (LB, 1), 0)
         valid = (t_at < length).astype(f32)
-        loss_ref[...] += jnp.sum(valid * (lt - pos))
+        gg_ref[3:4, :] += jnp.broadcast_to(jnp.sum(valid * (lt - pos), 0, keepdims=True), (1, D))
         d_pos = valid * inv * (jnp.exp(pos - lt) - 1.0)
         dn = (e * (valid * inv / total)).astype(bf16)
         dneg[r, :] = dn
@@ -284,14 +283,13 @@
             pl.BlockSpec((1, 1, L), lambda s: (s, 0, 0)),
             once(N, D), once(1, N), once(C, D), once(*gains.shape),
         ],
-        out_specs=[per, per, whole(C, D), whole(N, D), whole(8, D), whole(1, 1)],
+        out_specs=[per, per, whole(C, D), whole(N, D), whole(8, D)],
         out_shape=[
             jax.ShapeDtypeStruct((S, L, D), bf16),
             jax.ShapeDtypeStruct((S, L, D), bf16),
             jax.ShapeDtypeStruct((C, D), f32),
             jax.ShapeDtypeStruct((N, D), bf16),
             jax.ShapeDtypeStruct((8, D), f32),
-            jax.ShapeDtypeStruct((1, 1), f32),
         ],
         scratch_shapes=[
             V((L, D), f32), V((L, D), bf16), V((L, 3 * inner), bf16),
@@ -541,6 +539,514 @@
     return parts
 
 
+MESH = pl.DeviceIdType.MESH
+
+
+def round_up(n, unit):
+    return -(-n // unit) * unit
+
+
+def plan_kernel(rows_dev, ids_ref, rank_ref, owner_ref, slot_ref):
+    peers = slot_ref.shape[0]
+    lanes = slot_ref.shape[2]
+    P = ids_ref.shape[1]
+    KC = 256
+    low = lax.broadcasted_iota(jnp.int32, (peers, 1), 0) * rows_dev
+    upper = (
+        lax.broadcasted_iota(jnp.int32, (KC, KC), 0) < lax.broadcasted_iota(jnp.int32, (KC, KC), 1)
+    ).astype(f32).astype(bf16)
+    number = lax.broadcasted_iota(jnp.int32, (peers, 1), 0).astype(f32)
+    place = lax.broadcasted_iota(jnp.int32, (lanes, 1), 0)
+    carry = jnp.zeros((peers, 1), f32)
+    lists = jnp.zeros((3 * peers, lanes), f32)
+    for k in range(P // KC):
+        c = slice(k * KC, (k + 1) * KC)
+        ids = ids_ref[:, c]
+        own = jnp.logical_and(ids >= low, ids < low + rows_dev).astype(f32)
+        ahead = mm(own.astype(bf16), upper) + carry
+        rank = jnp.sum(own * ahead, 0, keepdims=True).astype(jnp.int32)
+        owner = jnp.sum(own * number, 0, keepdims=True).astype(jnp.int32)
+        carry = carry + jnp.sum(own, 1, keepdims=True)
+        rank_ref[:, c] = rank
+        owner_ref[:, c] = owner
+        local = ids - owner * rows_dev
+        high = lax.shift_right_logical(local, 6)
+        left = local - high * 64
+        coded = jnp.concatenate([own, own * left.astype(f32), own * high.astype(f32)], 0)
+        lists = lists + mm_t(coded.astype(bf16), (place == rank).astype(f32).astype(bf16))
+    there = lists[:peers] > 0.5
+    local = lists[peers : 2 * peers] + 64.0 * lists[2 * peers :]
+    out = jnp.where(there, local.astype(jnp.int32), -1)
+    for j in range(peers):
+        slot_ref[j] = out[j : j + 1]
+
+
+def plan(ids, rows_dev, peers, lanes):
+    P = ids.shape[1]
+    vm = pl.BlockSpec(memory_space=pltpu.VMEM)
+    return pl.pallas_call(
+        functools.partial(plan_kernel, rows_dev),
+        out_shape=[
+            jax.ShapeDtypeStruct((1, P), jnp.int32),
+            jax.ShapeDtypeStruct((1, P), jnp.int32),
+            jax.ShapeDtypeStruct((peers, 1, lanes), jnp.int32),
+        ],
+        in_specs=[vm],
+        out_specs=[vm, vm, vm],
+        compiler_params=pltpu.CompilerParams(vmem_limit_bytes=24 << 20),
+        name="plan",
+    )(ids)
+
+
+def xor3(a, b):
+    return sum(lax.rem(lax.div(a, m) + lax.div(b, m), 2) * m for m in (1, 2, 4))
+
+
+def reduce_kernel(
+    rows_dev, tail,
+    rank_ref, owner_ref, slot_ref, emb_ref, tgt_ref, negid_ref, neg_ref, grad_ref, stat_ref,
+    tab_ref, dense_ref, stat_out, tot_out,
+    R, stage, rb, idrb, Pacc, nrs, nst, nall, dco, dcr, dstg, drb, dmst, dmr, bst, brv, stc, str_, ssum, tst, trv,
+    s_row, r_row, s_id, r_id, s_nrs, r_nrs, s_nag, r_nag, s_dc, r_dc, s_d, r_d, s_dm, r_dm,
+    s_b, r_b, s_y, r_y, s_st, r_st, s_t, r_t, loc,
+):
+    g = lax.axis_index("grp")
+    row = lax.axis_index("row")
+    h = lax.div(row, 8)
+    pos = lax.rem(row, 8)
+    c = lax.rem(row, 2)
+    q_me = g * 4 + lax.div(pos, 2)
+    capr = stage.shape[2]
+    main = capr - tail
+    T = emb_ref.shape[0]
+    rp = tab_ref.shape[0]
+    W = 128
+    RC = rp
+    RZ = rp // 7
+    NC = rp // RC
+    NB = r_b.shape[0]
+    BR = rp // NB
+
+    def remote(src, dst, ss, rs, dev):
+        return pltpu.make_async_remote_copy(
+            src_ref=src, dst_ref=dst, send_sem=ss, recv_sem=rs, device_id=dev, device_id_type=MESH
+        )
+
+    def arrived(ref, sem):
+        pltpu.make_async_copy(ref, ref, sem).wait()
+
+    def cube(gg, pp):
+        return (gg, h * 8 + pp)
+
+    far = (g, (1 - h) * 8 + pos)
+
+    bar = pltpu.get_barrier_semaphore()
+    n_dev = 32
+    me = g * 16 + row
+
+    @pl.loop(1, n_dev)
+    def _(k):
+        o = lax.rem(me + k, n_dev)
+        pl.semaphore_signal(bar, inc=1, device_id=(lax.div(o, 16), lax.rem(o, 16)), device_id_type=MESH)
+    rank = rank_ref[...]
+
+    @pl.loop(0, capr // 16)
+    def _(i):
+        r0 = pl.multiple_of(i * 16, 16)
+        want = lax.broadcasted_iota(jnp.int32, (16, 1), 0) + r0
+        R[pl.ds(r0, 16), :] = (want == rank).astype(f32).astype(bf16)
+
+    KC = 1024
+
+    def build(step):
+        ph = lax.div(step, 8)
+        t = lax.rem(step, 8)
+        zh = h + (1 - ph) * (1 - 2 * h)
+        j = zh * 8 + xor3(pos, t)
+        acc = None
+        for k in range(2 * T // KC):
+            cols = slice(k * KC, (k + 1) * KC)
+            o = (owner_ref[:, cols] == j).astype(f32).astype(bf16)
+            src = emb_ref if k * KC < T else tgt_ref
+            r0 = (k * KC) % T
+            a = mm(R[:, cols] * o, src[r0:r0 + KC, :])
+            acc = a if acc is None else acc + a
+        stage[step, 0] = acc[:, :W].astype(bf16)
+        stage[step, 1] = acc[:, W:].astype(bf16)
+
+    def row_copies(step, yy):
+        ph = lax.div(step, 8)
+        t = lax.rem(step, 8)
+        zh = h + (1 - ph) * (1 - 2 * h)
+        p = xor3(pos, t)
+        at = t * 2 + g
+        return (
+            remote(stage.at[step, yy], rb.at[ph, at], s_row.at[step, yy], r_row.at[ph, at], cube(yy, p)),
+            remote(slot_ref.at[zh * 8 + p], idrb.at[ph, at], s_id.at[step, yy], r_id.at[ph, at], cube(yy, p)),
+        )
+
+    def self_copies(ph):
+        zh = h + (1 - ph) * (1 - 2 * h)
+        return (
+            pltpu.make_async_copy(stage.at[ph * 8, g], rb.at[ph, g], r_row.at[ph, g]),
+            pltpu.make_async_copy(slot_ref.at[zh * 8 + pos], idrb.at[ph, g], r_id.at[ph, g]),
+        )
+
+    def send(step):
+        for yy in range(2):
+            mine = jnp.logical_and(lax.rem(step, 8) == 0, g == yy)
+
+            @pl.when(jnp.logical_not(mine))
+            def _():
+                for cp in row_copies(step, yy):
+                    cp.start()
+
+            @pl.when(mine)
+            def _():
+                for cp in self_copies(lax.div(step, 8)):
+                    cp.start()
+
+    lines = lax.broadcasted_iota(jnp.int32, (RC, 1), 0)
+
+    def add_rows(ph, ids, vals):
+        @pl.loop(0, NC)
+        def _(i):
+            r0 = pl.multiple_of(i * RC, 16)
+            hot = (lines == (ids - r0)).astype(f32).astype(bf16)
+            Pacc[ph, pl.ds(r0, RC), :] += mm(hot, vals)
+
+    def receive(ph, t):
+        for gg in range(2):
+            at = t * 2 + gg
+            arrived(rb.at[ph, at], r_row.at[ph, at])
+            arrived(idrb.at[ph, at], r_id.at[ph, at])
+        i0 = idrb[ph, t * 2, :, :main]
+        i1 = idrb[ph, t * 2 + 1, :, :main]
+        v0 = rb[ph, t * 2, :main, :]
+        v1 = rb[ph, t * 2 + 1, :main, :]
+
+        @pl.loop(0, NC)
+        def _(i):
+            r0 = pl.multiple_of(i * RC, 16)
+            a = mm((lines == (i0 - r0)).astype(f32).astype(bf16), v0)
+            a = a + mm((lines == (i1 - r0)).astype(f32).astype(bf16), v1)
+            Pacc[ph, pl.ds(r0, RC), :] += a
+
+    def tails(ph):
+        lane = lax.broadcasted_iota(jnp.int32, (1, W), 1)
+        zh = h + (1 - ph) * (1 - 2 * h)
+        base = (zh * 8 + pos) * rows_dev
+        per = W // tail
+        for b in range(16 // per):
+            ids = jnp.full((1, W), -1, jnp.int32)
+            for k in range(per):
+                s = b * per + k
+                piece = idrb[ph, s, :, main:main + W]
+                if k:
+                    piece = pltpu.roll(piece, k * tail, 1)
+                ids = jnp.where(lax.div(lane, tail) == k, piece, ids)
+            vals = jnp.concatenate([rb[ph, b * per + k, main:, :] for k in range(per)], 0)
+            add_rows(ph, ids, vals)
+        NG = nall.shape[0]
+        for b in range(NG):
+            local = negid_ref[:, b * nall.shape[1]:(b + 1) * nall.shape[1]] - base
+            add_rows(ph, jnp.where(local < rows_dev, local, -1), nall[b])
+
+    @pl.loop(0, 2 * (rp // RZ))
+    def _(i):
+        r0 = pl.multiple_of(lax.rem(i, rp // RZ) * RZ, 16)
+        Pacc[lax.div(i, rp // RZ), pl.ds(r0, RZ), :] = jnp.zeros((RZ, W), f32)
+
+    build(0)
+    pl.semaphore_wait(bar, n_dev - 1)
+
+    core_copy = remote(grad_ref.at[:, 1 - c], dcr, s_dc, r_dc, (g, row + 1 - 2 * c))
+    core_copy.start()
+    own_copy = pltpu.make_async_copy(grad_ref.at[:, c], dco, loc.at[0])
+    own_copy.start()
+
+    nb = nrs.shape[1]
+
+    def nrs_copy(t):
+        p = xor3(pos, t)
+        return remote(neg_ref.at[pl.ds(pl.multiple_of(p * nb, 16), nb), :], nrs.at[t], s_nrs.at[t], r_nrs.at[t], cube(g, p))
+
+    @pl.loop(1, 8)
+    def _(t):
+        nrs_copy(t).start()
+
+    def stat_copy(k):
+        o = lax.rem(g * 8 + pos + k, 16)
+        return remote(stc, str_.at[g * 8 + pos], s_st.at[k], r_st.at[g * 8 + pos], cube(lax.div(o, 8), lax.rem(o, 8)))
+
+    def stat_from(k):
+        o = lax.rem(g * 8 + pos + k, 16)
+        arrived(str_.at[o], r_st.at[o])
+
+    stat_load = pltpu.make_async_copy(stat_ref, stc, loc.at[1])
+    stat_load.start()
+    stat_load.wait()
+    stat_own = pltpu.make_async_copy(stat_ref, str_.at[g * 8 + pos], loc.at[2])
+    stat_own.start()
+
+    @pl.loop(1, 16)
+    def _(k):
+        stat_copy(k).start()
+
+    def run(lo, hi):
+        @pl.loop(lo, hi)
+        def _(step):
+            build(step)
+            send(step - 1)
+
+    run(1, 4)
+
+    @pl.loop(1, 8)
+    def _(t):
+        arrived(nrs.at[t], r_nrs.at[t])
+    total = neg_ref[pl.ds(pl.multiple_of(pos * nb, 16), nb), :].astype(f32)
+    for t in range(1, 8):
+        total = total + nrs[t].astype(f32)
+    nst[0] = total[:, :W].astype(bf16)
+    nst[1] = total[:, W:].astype(bf16)
+
+    def nag_copy(t, yy):
+        p = xor3(pos, t)
+        return remote(
+            nst.at[yy], nall.at[g, pl.ds(pl.multiple_of(pos * nb, 16), nb), :],
+            s_nag.at[t, yy], r_nag.at[g, pos], cube(yy, p))
+
+    def nag_each(f_remote, f_self):
+        @pl.loop(0, 8)
+        def _(t):
+            for yy in range(2):
+                mine = jnp.logical_and(t == 0, g == yy)
+
+                @pl.when(jnp.logical_not(mine))
+                def _():
+                    f_remote(t, yy)
+
+                if f_self is not None:
+                    @pl.when(mine)
+                    def _():
+                        f_self()
+
+    def nag_self():
+        pltpu.make_async_copy(
+            nst.at[g], nall.at[g, pl.ds(pl.multiple_of(pos * nb, 16), nb), :], r_nag.at[g, pos]).start()
+
+    run(4, 5)
+    nag_each(lambda t, yy: nag_copy(t, yy).start(), nag_self)
+
+    run(5, 16)
+    send(jnp.int32(15))
+
+    core_copy.wait_recv()
+    own_copy.wait()
+    for q in range(8):
+        for hh in range(2):
+            idx = (q // 4) * 8 + (2 * hh + (q // 2) % 2) * 2 + q % 2
+            dstg[q, hh] = (dco[idx] + dcr[idx]).astype(bf16)
+
+    def d_copy(t):
+        q = xor3(q_me, t)
+        dev = (lax.div(q, 4), h * 8 + lax.rem(q, 4) * 2 + c)
+        return remote(dstg.at[q], drb.at[t], s_d.at[t], r_d.at[t], dev)
+
+    @pl.loop(1, 8)
+    def _(t):
+        d_copy(t).start()
+
+    @pl.loop(0, 8)
+    def _(t):
+        receive(0, t)
+
+    @pl.loop(0, 16)
+    def _(i):
+        gg = lax.div(i, 8)
+        pp = lax.rem(i, 8)
+        ref = nall.at[gg, pl.ds(pl.multiple_of(pp * nb, 16), nb), :]
+        arrived(ref, r_nag.at[gg, pp])
+    tails(0)
+
+    def b_copy(i):
+        ref = pl.ds(pl.multiple_of(i * BR, 16), BR)
+        return remote(bst.at[ref, :], brv.at[ref, :], s_b.at[i], r_b.at[i], far)
+
+    @pl.loop(0, NB)
+    def _(i):
+        ref = pl.ds(pl.multiple_of(i * BR, 16), BR)
+        bst[ref, :] = Pacc[0, ref, :].astype(bf16)
+
+        @pl.when(i > 0)
+        def _():
+            b_copy(i - 1).start()
+
+    b_copy(NB - 1).start()
+
+    stat_own.wait()
+
+    @pl.loop(1, 16)
+    def _(k):
+        stat_from(k)
+    half = str_[0]
+    for k in range(1, 16):
+        half = half + str_[k]
+    ssum[0] = half
+
+    @pl.loop(0, 7)
+    def _(t):
+        receive(1, t)
+
+    stat_far = remote(ssum.at[0], ssum.at[1], s_st.at[0], r_st.at[16], far)
+    stat_far.start()
+    receive(1, jnp.int32(7))
+
+    tails(1)
+
+    def y_copy(i):
+        ref = tab_ref.at[pl.ds(pl.multiple_of(i * BR, 16), BR), pl.ds(pl.multiple_of(g * W, W), W)]
+        return remote(ref, ref, s_y.at[i], r_y.at[i], (1 - g, row))
+
+    d_far = remote(dmst.at[1 - h], dmr, s_dm, r_dm, far)
+
+    def finish(i, sq):
+        rr = pl.ds(pl.multiple_of(i * BR, 16), BR)
+        arrived(brv.at[rr, :], r_b.at[i])
+        low = (Pacc[1, rr, :] + brv[rr, :].astype(f32)).astype(bf16)
+        tab_ref[rr, pl.ds(pl.multiple_of(g * W, W), W)] = low
+
+        @pl.when(i > 0)
+        def _():
+            y_copy(i - 1).start()
+        v = low.astype(f32)
+        return sq + jnp.sum(v * v, 0, keepdims=True)
+
+    sq = lax.fori_loop(0, NB - 1, finish, jnp.zeros((1, W), f32))
+
+    @pl.loop(1, 8)
+    def _(t):
+        arrived(drb.at[t], r_d.at[t])
+    both = dstg[q_me].astype(f32)
+    for t in range(1, 8):
+        both = both + drb[t].astype(f32)
+    dmst[...] = both.astype(bf16)
+    dense_ref[...] = jnp.where(h == 0, both[0], both[1])
+
+    d_far.start()
+    sq = finish(NB - 1, sq)
+    y_copy(NB - 1).start()
+    arrived(dmr, r_dm)
+    dense = dense_ref[...] + dmr[...].astype(f32)
+    dense_ref[...] = dense
+    dsq = jnp.sum(dense * dense, 0, keepdims=True)
+    tst[...] = sq + dsq[:, :W] + dsq[:, W:]
+
+    def t_copy(k):
+        o = lax.rem(me + k, n_dev)
+        return remote(tst, trv.at[me], s_t.at[k], r_t.at[me], (lax.div(o, 16), lax.rem(o, 16)))
+
+    t_own = pltpu.make_async_copy(tst, trv.at[me], loc.at[3])
+    t_own.start()
+
+    @pl.loop(1, n_dev)
+    def _(k):
+        t_copy(k).start()
+
+    arrived(ssum.at[1], r_st.at[16])
+    stat_out[...] = ssum[0] + ssum[1]
+    t_own.wait()
+
+    @pl.loop(1, n_dev)
+    def _(k):
+        o = lax.rem(me + k, n_dev)
+        arrived(trv.at[o], r_t.at[o])
+    tot = trv[0]
+    for k in range(1, n_dev):
+        tot = tot + trv[k]
+    tot_out[...] = tot
+
+    @pl.loop(0, NB)
+    def _(i):
+        ref = tab_ref.at[pl.ds(pl.multiple_of(i * BR, 16), BR), pl.ds(pl.multiple_of((1 - g) * W, W), W)]
+        arrived(ref, r_y.at[i])
+
+    core_copy.wait_send()
+    stat_far.wait_send()
+    d_far.wait_send()
+
+    @pl.loop(0, NB)
+    def _(i):
+        b_copy(i).wait_send()
+        y_copy(i).wait_send()
+
+    @pl.loop(1, 8)
+    def _(t):
+        nrs_copy(t).wait_send()
+        d_copy(t).wait_send()
+
+    @pl.loop(1, 16)
+    def _(k):
+        stat_copy(k).wait_send()
+
+    @pl.loop(1, n_dev)
+    def _(k):
+        t_copy(k).wait_send()
+
+    nag_each(lambda t, yy: nag_copy(t, yy).wait_send(), None)
+
+    @pl.loop(0, 16)
+    def _(step):
+        for yy in range(2):
+            mine = jnp.logical_and(lax.rem(step, 8) == 0, g == yy)
+
+            @pl.when(jnp.logical_not(mine))
+            def _():
+                for cp in row_copies(step, yy):
+                    cp.wait_send()
+
+
+def reduce_all(rank, owner, slots, emb, tgt, neg_ids, neg, grad, stat, rows_dev, cap, cid=1):
+    P = rank.shape[1]
+    T, D = emb.shape
+    W = 128
+    tail = 16
+    capr = (cap // 256) * 256 + tail
+    rp = round_up(rows_dev, 448)
+    lanes = slots.shape[2]
+    N = neg.shape[0]
+    nd = grad.shape[2]
+    NB = 4
+    V = pltpu.VMEM
+    DMA = pltpu.SemaphoreType.DMA
+    vm = pl.BlockSpec(memory_space=pltpu.VMEM)
+    any_ = pl.BlockSpec(memory_space=pl.ANY)
+    return pl.pallas_call(
+        functools.partial(reduce_kernel, rows_dev, tail),
+        out_shape=[
+            jax.ShapeDtypeStruct((rp, D), bf16),
+            jax.ShapeDtypeStruct((nd, D), f32),
+            jax.ShapeDtypeStruct((8, D), f32),
+            jax.ShapeDtypeStruct((1, W), f32),
+        ],
+        in_specs=[vm, vm, vm, vm, vm, vm, vm, any_, any_],
+        out_specs=[vm, vm, vm, vm],
+        scratch_shapes=[
+            V((capr, P), bf16), V((16, 2, capr, W), bf16), V((2, 16, capr, W), bf16), V((2, 16, 1, lanes), jnp.int32),
+            V((2, rp, W), f32), V((8, N // 8, D), bf16), V((2, N // 8, W), bf16), V((2, N, W), bf16),
+            V((16, nd, D), f32), V((16, nd, D), f32), V((8, 2, nd, D), bf16), V((8, 2, nd, D), bf16),
+            V((2, nd, D), bf16), V((nd, D), bf16), V((rp, W), bf16), V((rp, W), bf16),
+            V((8, D), f32), V((16, 8, D), f32), V((2, 8, D), f32), V((1, W), f32), V((32, 1, W), f32),
+            DMA((16, 2)), DMA((2, 16)), DMA((16, 2)), DMA((2, 16)), DMA((8,)), DMA((8,)), DMA((8, 2)), DMA((2, 8)),
+            DMA(()), DMA(()), DMA((8,)), DMA((8,)), DMA(()), DMA(()),
+            DMA((NB,)), DMA((NB,)), DMA((NB,)), DMA((NB,)), DMA((16,)), DMA((17,)), DMA((32,)), DMA((32,)), DMA((4,)),
+        ],
+        compiler_params=pltpu.CompilerParams(
+            collective_id=cid, has_side_effects=True, vmem_limit_bytes=58 * 1024 * 1024),
+        name="reduce_all",
+    )(rank, owner, slots, emb, tgt, neg_ids, neg, grad, stat)
+
+
 clip_level = 0.002
 adam_rate = 0.05
 gains_rate = 0.6
@@ -562,10 +1068,6 @@
     return (weight_new, first_new, second_new)
 
 
-def round_up(n, unit):
-    return -(-n // unit) * unit
-
-
 def digits(ints, base, count):
     return [((ints // base**k) % base).astype(bf16) for k in range(count)]
 
@@ -585,12 +1087,11 @@
     return v[:, 0], ids, events
 
 
-def slot_plan(requests, rows_dev, peers):
-    capacity = 2 * requests.shape[0] // peers
+def slot_plan(requests, rows_dev, peers, capacity):
     owners = requests // rows_dev
     one_hot = (owners[:, None] == jnp.arange(peers, dtype=jnp.int32)[None, :]).astype(jnp.int32)
     rank_in = jnp.sum((jnp.cumsum(one_hot, 0) - one_hot) * one_hot, 1)
-    return owners * capacity + rank_in, capacity
+    return owners * capacity + rank_in
 
 
 def exchange(blocks):
@@ -627,29 +1128,32 @@
     table_low = table_weight.astype(bf16)
     dense_low = dense_weight.T.astype(bf16)
     small = small_block(negative_ids, negative_logq, jnp.sum(lengths), width)
-    requests = jnp.concatenate([item_ids.reshape(-1), target_ids.reshape(-1), negative_ids])
-    slot_at, capacity = slot_plan(requests, rows_dev, peers)
-    send_ids = jnp.full((peers * capacity,), -1, jnp.int32).at[slot_at].set(requests)
-    asked_ids = exchange(send_ids.reshape(peers, capacity))
-    present = asked_ids >= 0
-
-    if (groups, X) == (2, 2):
+    event_ids = jnp.concatenate([item_ids.reshape(1, -1), target_ids.reshape(1, -1)], 1)
+    capacity = 2 * (event_ids.shape[1] + n_neg) // peers
+    kernels = (groups, peers) == (2, 16)
+
+    if kernels:
         rows_pad = round_up(rows_dev, 16)
         padded = jnp.pad(table_low, ((0, rows_pad - rows_dev), (0, 0)))
         table_all, dense_all, small_all = gather_all(
             padded, dense_low, small, Z, X, cut_parts(rows_pad, 2, 2, 0.333)
         )
-        neg_bias, neg_ids, event_total = read_small(small_all, n_neg)
-        neg_ids = lax.dynamic_slice_in_dim(neg_ids, g * peers, peers, 0).reshape(-1)
+        neg_bias, all_negs, event_total = read_small(small_all, n_neg)
+        neg_ids = lax.dynamic_slice_in_dim(all_negs, g * peers, peers, 0).reshape(1, -1)
         neg_bias = lax.dynamic_slice_in_dim(neg_bias, g * peers, peers, 0).reshape(1, -1)
-        wanted = jnp.concatenate([requests[: 2 * tokens], neg_ids])
+        wanted = jnp.concatenate([event_ids, neg_ids], 1)[0]
         wanted = wanted + (rows_pad - rows_dev) * (wanted // rows_dev)
         picked = table_all.reshape(peers * rows_pad, width)[wanted]
         neg_rows = picked[2 * tokens :]
     else:
+        requests = jnp.concatenate([event_ids[0], negative_ids])
+        slot_at = slot_plan(requests, rows_dev, peers, capacity)
+        send_ids = jnp.full((peers * capacity,), -1, jnp.int32).at[slot_at].set(requests)
+        asked_ids = exchange(send_ids.reshape(peers, capacity))
+        present = asked_ids >= 0
         dense_all = lax.all_gather(dense_low, ("grp", "row"), axis=0)
         small_all = lax.all_gather(small, ("grp", "row"), axis=0)
-        neg_bias, neg_ids, event_total = read_small(small_all, n_neg)
+        neg_bias, _, event_total = read_small(small_all, n_neg)
         neg_bias = lax.dynamic_slice_in_dim(neg_bias, g * peers, peers, 0).reshape(1, -1)
         found = table_low[jnp.where(present, asked_ids - row_base, 0)]
         found = jnp.where(present[..., None], found, jnp.zeros_like(found))
@@ -660,7 +1164,7 @@
     dense_all = dense_all.reshape(-1, width)
 
     inverse = 1.0 / event_total
-    d_embedded, d_target, grad_local, neg_local, gain_local, loss_local = seq_step(
+    d_embedded, d_target, grad_local, neg_local, stat_local = seq_step(
         lengths,
         inverse.reshape(1, 1),
         hist_rows,
@@ -671,26 +1175,33 @@
         dense_all,
         gain_weight,
     )
-    gain_local = gain_local[:3]
-
-    dense_grad = lax.psum_scatter(grad_local, ("grp", "row"), scatter_dimension=0, tiled=True).T
-    neg_grad = jnp.sum(exchange(neg_local.reshape(peers, n_neg, width)).astype(f32), 0)
-    row_grads = jnp.concatenate(
-        [d_embedded.reshape(tokens, width), d_target.reshape(tokens, width), neg_grad.astype(bf16)], 0
-    ).astype(f32)
-    sent = jnp.zeros((peers * capacity, width), f32).at[slot_at].set(row_grads).astype(bf16)
-    arrived = exchange(sent.reshape(peers, capacity, width)).astype(f32)
-    local_rows = jnp.where(present, asked_ids - row_base, 0).reshape(-1)
-    arrived = jnp.where(present[..., None], arrived, 0.0).reshape(-1, width)
-    owner_grad = jax.ops.segment_sum(arrived, local_rows, num_segments=rows_dev)
-    table_full = lax.psum(owner_grad.astype(bf16), "grp").astype(f32)
-
-    dense_sq = jnp.sum(dense_grad * dense_grad)
-    table_sq = jnp.sum(table_full * table_full) / groups
-    gain_grad, dense_total, table_total, loss_total = lax.psum(
-        (gain_local, dense_sq, table_sq, loss_local[0, 0]), ("grp", "row")
-    )
-    raw_norm = jnp.sqrt(dense_total + table_total + jnp.sum(gain_grad * gain_grad))
+    d_embedded = d_embedded.reshape(tokens, width)
+    d_target = d_target.reshape(tokens, width)
+
+    if kernels:
+        rank, owner, lists = plan(event_ids, rows_dev, peers, round_up(capacity, 128))
+        table_full, dense_grad, stats, squares = reduce_all(
+            rank, owner, lists, d_embedded, d_target, all_negs.reshape(1, -1), neg_local,
+            grad_local.reshape(groups * peers // 2, 2, -1, width), stat_local, rows_dev, capacity,
+        )
+        table_full = table_full[:rows_dev].astype(f32)
+        dense_grad = dense_grad.T
+        squares = jnp.sum(squares)
+    else:
+        dense_grad = lax.psum_scatter(grad_local, ("grp", "row"), scatter_dimension=0, tiled=True).T
+        neg_grad = jnp.sum(exchange(neg_local.reshape(peers, n_neg, width)).astype(f32), 0)
+        row_grads = jnp.concatenate([d_embedded, d_target, neg_grad.astype(bf16)], 0).astype(f32)
+        sent = jnp.zeros((peers * capacity, width), f32).at[slot_at].set(row_grads).astype(bf16)
+        arrived = exchange(sent.reshape(peers, capacity, width)).astype(f32)
+        local_rows = jnp.where(present, asked_ids - row_base, 0).reshape(-1)
+        arrived = jnp.where(present[..., None], arrived, 0.0).reshape(-1, width)
+        owner_grad = jax.ops.segment_sum(arrived, local_rows, num_segments=rows_dev)
+        table_full = lax.psum(owner_grad.astype(bf16), "grp").astype(f32)
+        squares = jnp.sum(dense_grad * dense_grad) + jnp.sum(table_full * table_full) / groups
+        stats, squares = lax.psum((stat_local, squares), ("grp", "row"))
+    gain_grad = stats[:3]
+    loss_total = stats[3, 0]
+    raw_norm = jnp.sqrt(squares + jnp.sum(gain_grad * gain_grad))
     factor = jnp.minimum(1.0, clip_level / raw_norm)
     table_grad = table_full * factor
     new_accum = table_accum + jnp.mean(table_grad * table_grad, -1)

time: 654 us -> 434 us (0.66)
  waiting for transfers between devices: 162 us -> 0 us
  Pallas kernels: 233 us -> 363 us
  other arithmetic: 119 us -> 17.8 us
  blocking collectives: 39.6 us -> 0 us
  starting transfers between devices: 17.7 us -> 0 us
  local copies, waits for them, and re-layouts: 55.3 us -> 38.8 us
  between operations: 25.6 us -> 9.45 us
    pallas_call x0 -> x2, Pallas kernels: none -> 130 us  [the longest x1 126 us: reduce_all(): pl.pallas_call(functools.partial(reduce_kernel, rows_dev, tail), out_shap...]
    all_to_all x3 -> x0, waiting for transfers between devices: 90.4 us -> none  [exchange(): lax.all_to_all(blocks, 'row', split_axis=0, concat_axis=0, tiled=True)]
    psum x1 -> x0, waiting for transfers between devices: 71.2 us -> none  [shards(): table_full = lax.psum(owner_grad.astype(bf16), 'grp').astype(f32)]
    scatter-add x1 -> x0, other arithmetic: 52.6 us -> none  [shards(): owner_grad = jax.ops.segment_sum(arrived, local_rows, num_segments=rows_dev)]
    psum x1 -> x0, blocking collectives: 39.6 us -> none  [shards(): lax.psum((gain_local, dense_sq, table_sq, loss_local[0, 0]), ('grp', 'row'))]
    scatter x1 -> x0, other arithmetic: 31.3 us -> none  [shards(): jnp.zeros((peers * capacity, width), f32).at[slot_at].set(row_grads)]
    scatter x1 -> x0, local copies, waits for them, and re-layouts: 20.6 us -> none  [shards(): jnp.full((peers * capacity,), -1, jnp.int32).at[slot_at].set(requests)]
    all_to_all x3 -> x0, starting transfers between devices: 17.7 us -> none  [exchange(): lax.all_to_all(blocks, 'row', split_axis=0, concat_axis=0, tiled=True)]
  transfers between devices with their start and end apart: 5 -> 0, of which waited for: 2 -> 0; matrix products, arithmetic and copies ran while one was open for 19% -> 0% of each run, Pallas kernels for 0% -> 0%
where the time goes in v2:
time: 434 us; the launch traced here: 429 us
  Pallas kernels  363 us (84%)
  local copies, waits for them, and re-layouts  38.8 us (9%)
  other arithmetic  17.8 us (4%)
  between operations  9.45 us (2%)
    pallas_call x1, Pallas kernels, reduce_all(): pl.pallas_call(functools.partial(reduce_kernel, rows_dev, tail), out_shap...  126 us
    pallas_call x1, Pallas kernels, gather_all(): pl.pallas_call(functools.partial(gather_kernel, Z, X, parts), out_shape=[...  118 us
    pallas_call x1, Pallas kernels, seq_step(): pl.pallas_call(seq_kernel, grid=(S,), in_specs=[pl.BlockSpec(memory_space...  115 us
    gather x1, local copies, waits for them, and re-layouts, shards(): picked = table_all.reshape(peers * rows_pad, width)[wanted]  28.3 us

profile of v2, /device:TPU:0, one launch (start us, length us, event | category | flops | bytes accessed | tf_op | source)
XLA Modules:
  0.0 428.8 jit_solution(16841415181689664180)
XLA Ops:
  0.6 1.3 reduce_sum.45
  4.6 0.7 fusion.13
  5.3 0.7 stack.19
  6.0 0.7 copy.27
  6.7 0.7 copy.28
  7.4 1.3 reshape.206.tlq_ref
  8.7 3.9 plan.1
  12.6 0.9 convert_bitcast_fusion.wts
  13.5 2.1 convert_element_type.54
  15.6 0.1 pad.8.tab
  15.8 118.0 %gather_all.1 = (bf16[16,3136,256]{2,1,0:T(8,128)(2,1)}, bf16[32,144,256]{2,1,0:T(8,128)(2,1)S(1)}, bf16[32,16,256]{2,1,0:T(8,128)(2,1)S(1)}) custom-call(bf16[3136,256]{1,0:T(8,128)(2,1)S(1)} %pad.8.tab, bf16[144,256]{1,0:T(8,128)(2,1)S(1)} %convert_bitcast_fusion.wts, bf16[16,256]{1,0:T(8,128)(2,1)S(1)} %pad.9.meta), custom_call_target="tpu_custom_call" | custom-call | tf_op jit(solution)/shard_map/gather_all/pallas_call | solution.py:507
  133.7 1.4 copy-done
  135.1 0.6 fusion.5
  136.5 0.5 broadcast.171
  137.0 0.7 fusion.21
  137.8 0.7 reshape.200.nlq_ref
  138.5 0.7 convert_element_type.64.negid_ref
  139.2 0.1 reshape.195
  139.2 0.2 compare_select_fusion
  139.4 28.3 %gather_fusion = bf16[5120,256]{1,0:T(8,128)(2,1)S(1)} fusion(bf16[50176,256]{1,0:T(8,128)(2,1)} %bitcast.37, s32[5120]{0:T(1024)S(1)} %broadcast_clamp_fusion), kind=kCustom, calls=%fused_computation | custom fusion | bytes 5263360 | tf_op jit(solution)/shard_map/gather | solution.py:1146
  167.7 0.8 slice.61.neg_ref
  168.6 1.4 fusion.23
  170.0 115.2 %seq_step.1 = (bf16[4,512,256]{2,1,0:T(8,128)(2,1)}, bf16[4,512,256]{2,1,0:T(8,128)(2,1)}, f32[4608,256]{1,0:T(8,128)}, bf16[1024,256]{1,0:T(8,128)(2,1)}, f32[8,256]{1,0:T(8,128)}) custom-call(s32[4]{0:T(128)} %len_ref.1, f32[1,1]{1,0:T(1,128)} %bitcast.5.inv_ref, bf16[4,512,256]{2,1,0:T(8,128)(2,1)} %bitcast.40, bf16[4,512,256]{2,1,0:T(8,128)(2,1)} %bitcast.39, ...), custom_call_target="tpu_custom_call" | custom-call | tf_op jit(solution)/shard_map/seq_step/pallas_call | solution.py:276
  285.3 125.7 %reduce_all.1 = (bf16[3136,256]{1,0:T(8,128)(2,1)}, f32[144,256]{1,0:T(8,128)}, f32[8,256]{1,0:T(8,128)}, f32[1,128]{1,0:T(1,128)}) custom-call(s32[1,4096]{1,0:T(1,128)} %copy-done.2, s32[1,4096]{1,0:T(1,128)} %copy-done.3, s32[16,1,640]{2,1,0:T(1,128)} %copy-done.1, bf16[2048,256]{1,0:T(8,128)(2,1)} %bitcast.41, bf16[2048,256]{1,0:T(8,128)(2,1)} %bitcast.42, ...), custom_call_target="tpu_custom_call" | custom-call | tf_op jit(solution)/shard_map/reduce_all/pallas_call | solution.py:1024
  411.1 1.5 multiply_reduce_fusion.1
  412.5 1.2 slice.49
  415.0 1.2 reduce_sum.47
  417.7 1.3 multiply_subtract_fusion.1
  419.0 1.8 fusion.17
  420.8 1.9 multiply_reduce_fusion
  422.8 0.7 sqrt_add_fusion
  423.5 2.9 fusion.20
  (32 shorter events, 0.2 us)
Async XLA Ops:
  12.6 3.0 copy-start.1
  12.6 3.0 copy-start.2
  12.6 3.0 copy-start.3
  133.7 1.4 copy-start
  285.3 132.4 %copy-start.9 = (f32[3,256]{1,0:T(4,128)S(1)}, f32[3,256]{1,0:T(4,128)}, u32[]{:S(2)}) copy-start(f32[3,256]{1,0:T(4,128)} %gain_ref.1) | copy-start | bytes 9220
  285.3 132.4 %copy-start.10 = (f32[3,256]{1,0:T(4,128)S(1)}, f32[3,256]{1,0:T(4,128)}, u32[]{:S(2)}) copy-start(f32[3,256]{1,0:T(4,128)} %param.26) | copy-start | bytes 9220
  285.3 132.4 %copy-start.11 = (f32[3,256]{1,0:T(4,128)S(1)}, f32[3,256]{1,0:T(4,128)}, u32[]{:S(2)}) copy-start(f32[3,256]{1,0:T(4,128)} %param.27) | copy-start | bytes 9220
  285.3 133.7 %copy-start.6 = (f32[256,144]{0,1:T(8,128)S(1)}, f32[256,144]{0,1:T(8,128)}, u32[]{:S(2)}) copy-start(f32[256,144]{0,1:T(8,128)} %param.22) | copy-start | bytes 442372
  285.3 133.7 %copy-start.7 = (f32[256,144]{0,1:T(8,128)S(1)}, f32[256,144]{0,1:T(8,128)}, u32[]{:S(2)}) copy-start(f32[256,144]{0,1:T(8,128)} %param.23) | copy-start | bytes 442372
  411.0 11.8 %copy-start.8 = (f32[3125]{0:T(1024)S(1)}, f32[3125]{0:T(1024)}, u32[]{:S(2)}) copy-start(f32[3125]{0:T(1024)} %param.21) | copy-start | bytes 37504
  411.0 12.4 %copy-start.4 = (f32[3125,256]{1,0:T(8,128)S(1)}, f32[3125,256]{1,0:T(8,128)}, u32[]{:S(2)}) copy-start(f32[3125,256]{1,0:T(8,128)} %param.20) | copy-start | bytes 9600004
  422.8 3.6 copy-start.5
